TPU v7x, 32 devices: a whole 2x2x4 slice. The times are simulated.
32 devices in a mesh: seq: 8 (over z, x), head: 4 (over y, core).
Axes of the slice: x: 2, y: 2, z: 4, core: 2. Of those that a mesh axis runs over, the one named last changes fastest.
Arguments:
- block_input: float32 [1, 2048, 1536], P(None, 'seq'), may hold values from -6 to 6
- cotangent: float32 [1, 2048, 1536], P(None, 'seq'), may hold values from -6 to 6
- gate_proj: float32 [1536, 3072], P('seq', 'head'), may hold values from -0.15625 to 0.15625
- value_proj: float32 [1536, 3072], P('seq', 'head'), may hold values from -0.15625 to 0.15625
- bc_proj: float32 [1536, 256], P('seq'), may hold values from -0.15625 to 0.15625
- step_proj: float32 [1536, 48], P('seq', 'head'), may hold values from -0.15625 to 0.15625
- out_proj: float32 [3072, 1536], P('head', 'seq'), may hold values from -0.109375 to 0.109375
- in_gain: float32 [1536], replicated, may hold values from 0.5 to 1.5
- conv_value: float32 [5, 3072], replicated, may hold values from -3 to 3
- conv_bc: float32 [5, 256], replicated, may hold values from -3 to 3
- head_params: float32 [3, 48], replicated, as said below
- out_gain: float32 [3072], replicated, may hold values from 0.5 to 1.5
- m_gate: float32 [1536, 3072], P('seq', 'head'), may hold values from -24 to 24
- m_value: float32 [1536, 3072], P('seq', 'head'), may hold values from -24 to 24
- m_bc: float32 [1536, 256], P('seq'), may hold values from -24 to 24
- m_step: float32 [1536, 48], P('seq', 'head'), may hold values from -24 to 24
- m_out: float32 [3072, 1536], P('head', 'seq'), may hold values from -24 to 24
- m_ingain: float32 [1536], replicated, may hold values from -6 to 6
- m_convvalue: float32 [5, 3072], replicated, may hold values from -6 to 6
- m_convbc: float32 [5, 256], replicated, may hold values from -6 to 6
- m_head: float32 [3, 48], replicated, may hold values from -6 to 6
- m_outgain: float32 [3072], replicated, may hold values from -6 to 6
Outputs:
- block_output: float32 [1, 2048, 1536], P(None, 'seq', 'head')
- input_grad: float32 [1, 2048, 1536], P(None, 'seq', 'head')
- grad_gate: float32 [1536, 3072], P('seq', 'head')
- grad_value: float32 [1536, 3072], P('seq', 'head')
- grad_bc: float32 [1536, 256], P('seq')
- grad_step: float32 [1536, 48], P('seq', 'head')
- grad_out: float32 [3072, 1536], P('head', 'seq')
- grad_ingain: float32 [1536], replicated
- grad_convvalue: float32 [5, 3072], replicated
- grad_convbc: float32 [5, 256], replicated
- grad_head: float32 [3, 48], replicated
- grad_outgain: float32 [3072], replicated
- new_gate: float32 [1536, 3072], P('seq', 'head')
- new_value: float32 [1536, 3072], P('seq', 'head')
- new_bc: float32 [1536, 256], P('seq')
- new_step: float32 [1536, 48], P('seq', 'head')
- new_out: float32 [3072, 1536], P('head', 'seq')
- new_ingain: float32 [1536], replicated
- new_convvalue: float32 [5, 3072], replicated
- new_convbc: float32 [5, 256], replicated
- new_head: float32 [3, 48], replicated
- new_outgain: float32 [3072], replicated
- next_gate: float32 [1536, 3072], P('seq', 'head')
- next_value: float32 [1536, 3072], P('seq', 'head')
- next_bc: float32 [1536, 256], P('seq')
- next_step: float32 [1536, 48], P('seq', 'head')
- next_out: float32 [3072, 1536], P('head', 'seq')
- next_ingain: float32 [1536], replicated
- next_convvalue: float32 [5, 3072], replicated
- next_convbc: float32 [5, 256], replicated
- next_head: float32 [3, 48], replicated
- next_outgain: float32 [3072], replicated
Inputs may be any that keep to these rules, and one draw needn't show every extreme that they name: `head_params`: row 0 is each head's logarithm of its decay rate, row 1 its skip gain, row 2 the bias of its step size.
All inputs are finite; a program needn't handle non-finite values.
Results may differ from a plain program's by a relative error of at most 0.0003.
Values sent between devices are 32-bit elements; how exact they have to be, the bound alone decides.
A program may use at most 192 MiB of HBM per device.

v0:
```python
import math

import jax
import jax.numpy as jnp
from jax import lax
from jax.sharding import PartitionSpec as P

D = 1536
DI = 3072
STATE = 128
H = 48
GROUP = 256
CONV = 4
SWEEPS = 5


HIGHEST = lax.Precision.HIGHEST
EPSILON = 1e-05
QUINTIC_A = 3.4445
QUINTIC_B = -4.775
QUINTIC_C = 2.0315
MOMENTUM_KEEP = 0.9
MATRIX_RATE = 0.02
VECTOR_RATE = 0.002
MUON_SCALE = 0.2


def from_behind(value, axis, steps):
    count = lax.axis_size(axis)
    initial, last = (max(0, -steps), min(count, count - steps))
    return lax.ppermute(value, axis, [(source, source + steps) for source in range(initial, last)])


def carried_in(part, axis, combine, identity, reverse):
    count = lax.axis_size(axis)
    place = lax.axis_index(axis)
    ahead = count - 1 - place if reverse else place
    gathered = jax.tree.map(lambda a: lax.all_gather(a, axis), part)
    state = jax.tree.map(lambda a, e: jnp.zeros_like(a) + jnp.asarray(e, a.dtype), part, identity)

    def one(turn, state):
        source = count - 1 - turn if reverse else turn
        return combine(
            state, jax.tree.map(lambda a: lax.dynamic_index_in_dim(a, source, 0, False), gathered)
        )

    return lax.fori_loop(0, ahead, one, state)


def silu_grad(pre_value):
    sigmoid_val = jax.nn.sigmoid(pre_value)
    return sigmoid_val * (1.0 + pre_value * (1.0 - sigmoid_val))


def project(activation, weight):
    return jnp.einsum("std,dk->stk", activation, weight, precision=HIGHEST)


def back_project(upstream, weight):
    return jnp.einsum("stk,dk->std", upstream, weight, precision=HIGHEST)


def weight_grad(activation, upstream):
    return jnp.einsum("std,stk->dk", activation, upstream, precision=HIGHEST)


def place_slice(portion, full_size, offset, along):
    full_shape = list(portion.shape)
    full_shape[along] = full_size
    return lax.dynamic_update_slice_in_dim(
        jnp.zeros(full_shape, jnp.float32), portion, offset, along
    )


def running_decay(log_decay):
    seq_count, tokens, head_count = log_decay.shape
    blocks = tokens // GROUP
    grouped = log_decay.reshape(seq_count, blocks, GROUP, head_count)
    rows_at = lax.broadcasted_iota(jnp.int32, (GROUP, GROUP), 0)
    cols_at = lax.broadcasted_iota(jnp.int32, (GROUP, GROUP), 1)
    lower_mask = rows_at >= cols_at
    within = jnp.einsum("ij,sbjh->sbih", lower_mask.astype(jnp.float32), grouped, precision=HIGHEST)
    group_total = within[:, :, -1, :]
    through = jnp.cumsum(group_total, axis=1)
    before = through - group_total
    return (lower_mask, within, group_total, through, before)


def group_core(values, step_size, log_decay, b_state, c_state, skip_gain):
    seq_count, tokens, width = values.shape
    head_count = step_size.shape[2]
    head_dim = width // head_count
    blocks = tokens // GROUP
    lower_mask, within, group_total, through, before = running_decay(log_decay)
    head_values = values.reshape(seq_count, blocks, GROUP, head_count, head_dim)
    step_blocks = step_size.reshape(seq_count, blocks, GROUP, head_count)
    b_blocks = b_state.reshape(seq_count, blocks, GROUP, -1)
    c_blocks = c_state.reshape(seq_count, blocks, GROUP, -1)
    decay_rows = within.transpose(0, 1, 3, 2)
    log_gaps = decay_rows[..., :, None] - decay_rows[..., None, :]
    decay_mat = jnp.where(lower_mask, jnp.exp(jnp.where(lower_mask, log_gaps, 0.0)), 0.0)
    scores = jnp.einsum("sbin,sbjn->sbij", c_blocks, b_blocks, precision=HIGHEST)
    weighted = scores[:, :, None] * decay_mat * step_blocks.transpose(0, 1, 3, 2)[:, :, :, None, :]
    intra_out = jnp.einsum("sbhij,sbjhp->sbihp", weighted, head_values, precision=HIGHEST)
    to_end = jnp.exp(group_total[:, :, None, :] - within) * step_blocks
    states = jnp.einsum("sbjh,sbjhp,sbjn->sbhpn", to_end, head_values, b_blocks, precision=HIGHEST)
    later_at = lax.broadcasted_iota(jnp.int32, (blocks, blocks), 0)
    earlier_at = lax.broadcasted_iota(jnp.int32, (blocks, blocks), 1)
    earlier_mask = (later_at > earlier_at)[None, :, :, None]
    carry_gap = before[:, :, None, :] - through[:, None, :, :]
    carry_factor = jnp.where(earlier_mask, jnp.exp(jnp.where(earlier_mask, carry_gap, 0.0)), 0.0)
    entering = jnp.einsum("skmh,smhpn->skhpn", carry_factor, states, precision=HIGHEST)
    inter_out = (
        jnp.einsum("sbin,sbhpn->sbihp", c_blocks, entering, precision=HIGHEST)
        * jnp.exp(within)[..., None]
    )
    output = intra_out + inter_out + skip_gain[:, None] * head_values
    end_gap = through - through
    summary = jnp.einsum("sbh,sbhpn->shpn", jnp.exp(end_gap), states, precision=HIGHEST)
    decay_all = jnp.exp(through[:, -1, :])
    return (output.reshape(seq_count, tokens, width), decay_all, summary)


def entry_term(entry_state, log_decay, c_state):
    seq_count, tokens, head_count = log_decay.shape
    blocks = tokens // GROUP
    _, within, _, _, before = running_decay(log_decay)
    reach = jnp.exp(within + before[:, :, None, :])
    c_blocks = c_state.reshape(seq_count, blocks, GROUP, -1)
    result = (
        jnp.einsum("sbin,shpn->sbihp", c_blocks, entry_state, precision=HIGHEST) * reach[..., None]
    )
    return result.reshape(seq_count, tokens, -1)


def full_mixer(values, step_size, log_decay, b_state, c_state, skip_gain, entry_state):
    base_out, decay_all, summary = group_core(
        values, step_size, log_decay, b_state, c_state, skip_gain
    )
    output = base_out + entry_term(entry_state, log_decay, c_state)
    leaving = decay_all[..., None, None] * entry_state + summary
    return (output, leaving)


def combine_states(earlier, later):
    return (earlier[0] * later[0], later[0][..., None, None] * earlier[1] + later[1])


def gramian(matrix):
    return jnp.dot(matrix, matrix.T, precision=HIGHEST)


def on_device(
    block_input,
    cotangent,
    gate_proj,
    value_proj,
    bc_proj,
    step_proj,
    out_proj,
    in_gain,
    conv_value,
    conv_bc,
    head_params,
    out_gain,
    m_gate,
    m_value,
    m_bc,
    m_step,
    m_out,
    m_ingain,
    m_convvalue,
    m_convbc,
    m_head,
    m_outgain,
):
    head_count = lax.axis_size("head")
    head_index = lax.axis_index("head")
    seq_index = lax.axis_index("seq")
    seq_count, tokens, _ = block_input.shape
    row_count = gate_proj.shape[0]
    inner_width = gate_proj.shape[1]
    local_heads = step_proj.shape[1]
    bc_width = 2 * STATE // head_count
    model_part = D // head_count
    gate_full, value_full, bc_full, step_full, out_full = (
        lax.all_gather(gate_proj, "seq", axis=0, tiled=True),
        lax.all_gather(value_proj, "seq", axis=0, tiled=True),
        lax.all_gather(bc_proj, "seq", axis=0, tiled=True),
        lax.all_gather(step_proj, "seq", axis=0, tiled=True),
        lax.all_gather(out_proj, "seq", axis=1, tiled=True),
    )
    conv_mine = lax.dynamic_slice_in_dim(conv_value, head_index * inner_width, inner_width, 1)
    gain_mine = lax.dynamic_slice_in_dim(out_gain, head_index * inner_width, inner_width, 0)
    head_mine = lax.dynamic_slice_in_dim(head_params, head_index * local_heads, local_heads, 1)
    bc_cols = lax.dynamic_slice_in_dim(bc_full, head_index * bc_width, bc_width, 1)
    bc_taps = lax.dynamic_slice_in_dim(conv_bc, head_index * bc_width, bc_width, 1)
    inv_rms = lax.rsqrt(jnp.mean(block_input * block_input, axis=-1, keepdims=True) + EPSILON)
    normed = block_input * inv_rms * in_gain
    gate_pre = project(normed, gate_full)
    mixed_pre = jnp.concatenate([project(normed, value_full), project(normed, bc_cols)], axis=-1)
    step_pre = project(normed, step_full)
    conv_taps = jnp.concatenate([conv_mine, bc_taps], axis=-1)
    edge_rows = from_behind(mixed_pre[:, tokens - (CONV - 1) :, :], "seq", 1)
    padded = jnp.concatenate([edge_rows, mixed_pre], axis=1)
    conv_out = conv_taps[CONV] + sum(
        (conv_taps[offset] * padded[:, offset : offset + tokens, :] for offset in range(CONV))
    )
    activated = jax.nn.silu(conv_out)
    values = activated[..., :inner_width]
    bc_all = lax.all_gather(activated[..., inner_width:], "head", axis=2, tiled=True)
    b_state = bc_all[..., :STATE]
    c_state = bc_all[..., STATE:]
    decay_rate = jnp.exp(head_mine[0])
    skip_gain = head_mine[1]
    step_arg = step_pre + head_mine[2]
    step_size = jax.nn.softplus(step_arg)
    log_decay = -decay_rate * step_size
    base_out, decay_all, summary = group_core(
        values, step_size, log_decay, b_state, c_state, skip_gain
    )
    scan_start = (jnp.ones_like(decay_all), jnp.zeros_like(summary))
    _, entry_state = carried_in((decay_all, summary), "seq", combine_states, scan_start, False)
    mixer_out = base_out + entry_term(entry_state, log_decay, c_state)
    gate_act = jax.nn.silu(gate_pre)
    gated = mixer_out * gate_act
    square_part = jnp.sum(gated * gated, axis=-1, keepdims=True)
    square_rep = jnp.broadcast_to(square_part, (seq_count, tokens, head_count))
    out_part = project(gated * gain_mine, out_full)
    out_sum, square_sum = (
        lax.psum_scatter(out_part, "head", scatter_dimension=2, tiled=True),
        lax.psum_scatter(square_rep, "head", scatter_dimension=2, tiled=True),
    )
    gate_rms = lax.rsqrt(square_sum / DI + EPSILON)
    input_mine = lax.dynamic_slice_in_dim(block_input, head_index * model_part, model_part, 2)
    cotangent_mine = lax.dynamic_slice_in_dim(cotangent, head_index * model_part, model_part, 2)
    block_output = input_mine + gate_rms * out_sum
    normed_out = gated * gate_rms * gain_mine
    grad_outproj = jnp.einsum("stc,std->cd", normed_out, cotangent, precision=HIGHEST)
    grad_normout = jnp.einsum("std,cd->stc", cotangent, out_full, precision=HIGHEST)
    grad_outgain_mine = jnp.sum(grad_normout * gated * gate_rms, axis=(0, 1))
    scaled = grad_normout * gain_mine
    dot_total = lax.psum(jnp.sum(scaled * gated, axis=-1, keepdims=True), "head")
    grad_gated = gate_rms * scaled - gate_rms**3 * gated * dot_total / DI
    grad_mixer = grad_gated * gate_act
    grad_gate_pre = grad_gated * mixer_out * silu_grad(gate_pre)
    _, entry_back = jax.vjp(lambda entering: entry_term(entering, log_decay, c_state), entry_state)
    direct = entry_back(grad_mixer)[0]
    _, leave_grad = carried_in((decay_all, direct), "seq", combine_states, scan_start, True)
    _, mixer_back = jax.vjp(
        full_mixer, values, step_size, log_decay, b_state, c_state, skip_gain, entry_state
    )
    grad_values, grad_stepsize, grad_logdecay, grad_b, grad_c, grad_skip, _ = mixer_back(
        (grad_mixer, leave_grad)
    )
    grad_step_total = grad_stepsize - grad_logdecay * decay_rate
    grad_alog = jnp.sum(grad_logdecay * log_decay, axis=(0, 1))
    grad_step_pre = grad_step_total * jax.nn.sigmoid(step_arg)
    grad_bias = jnp.sum(grad_step_pre, axis=(0, 1))
    grad_bc_all = jnp.concatenate([grad_b, grad_c], axis=-1)
    grad_bc_act = lax.psum_scatter(grad_bc_all, "head", scatter_dimension=2, tiled=True)
    grad_conv = jnp.concatenate([grad_values, grad_bc_act], axis=-1) * silu_grad(conv_out)
    grad_taps = jnp.stack(
        [
            jnp.sum(grad_conv * padded[:, offset : offset + tokens, :], axis=(0, 1))
            for offset in range(CONV)
        ]
        + [jnp.sum(grad_conv, axis=(0, 1))]
    )
    grad_padded = sum(
        (
            jnp.pad(conv_taps[offset] * grad_conv, ((0, 0), (offset, CONV - 1 - offset), (0, 0)))
            for offset in range(CONV)
        )
    )
    edge_back = from_behind(grad_padded[:, : CONV - 1, :], "seq", -1)
    grad_mixed = grad_padded[:, CONV - 1 :, :] + jnp.pad(
        edge_back, ((0, 0), (tokens - (CONV - 1), 0), (0, 0))
    )
    grad_value_pre = grad_mixed[..., :inner_width]
    grad_bc_pre = grad_mixed[..., inner_width:]
    grad_normed = (
        back_project(grad_gate_pre, gate_full)
        + back_project(grad_value_pre, value_full)
        + back_project(grad_bc_pre, bc_cols)
        + back_project(grad_step_pre, step_full)
    )
    stat_part = jnp.sum(grad_normed * in_gain * block_input, axis=-1, keepdims=True)
    stat_rep = jnp.broadcast_to(stat_part, (seq_count, tokens, head_count))
    normed_grad_mine, stat_total = (
        lax.psum_scatter(grad_normed, "head", scatter_dimension=2, tiled=True),
        lax.psum_scatter(stat_rep, "head", scatter_dimension=2, tiled=True),
    )
    gain_part = lax.dynamic_slice_in_dim(in_gain, head_index * model_part, model_part, 0)
    input_grad = (
        cotangent_mine
        + inv_rms * gain_part * normed_grad_mine
        - inv_rms**3 * input_mine * stat_total / D
    )
    grad_ingain_mine = jnp.sum(normed_grad_mine * input_mine * inv_rms, axis=(0, 1))
    grad_gatefull = weight_grad(normed, grad_gate_pre)
    grad_valuefull = weight_grad(normed, grad_value_pre)
    grad_stepfull = weight_grad(normed, grad_step_pre)
    grad_bclocal = weight_grad(normed, grad_bc_pre)
    grad_bcspread = place_slice(grad_bclocal, 2 * STATE, head_index * bc_width, 1)
    grad_convbc_spread = place_slice(
        grad_taps[:, inner_width:], 2 * STATE, head_index * bc_width, 1
    )
    grad_convvalue_spread = place_slice(grad_taps[:, :inner_width], DI, head_index * inner_width, 1)
    grad_head_spread = place_slice(
        jnp.stack([grad_alog, grad_skip, grad_bias]), H, head_index * local_heads, 1
    )
    grad_ingain_spread = place_slice(grad_ingain_mine, D, head_index * model_part, 0)
    grad_outgain_spread = place_slice(grad_outgain_mine, DI, head_index * inner_width, 0)
    grad_gate, grad_value, grad_step, grad_out = (
        lax.psum_scatter(grad_gatefull, "seq", scatter_dimension=0, tiled=True),
        lax.psum_scatter(grad_valuefull, "seq", scatter_dimension=0, tiled=True),
        lax.psum_scatter(grad_stepfull, "seq", scatter_dimension=0, tiled=True),
        lax.psum_scatter(grad_outproj, "seq", scatter_dimension=1, tiled=True),
    )
    grad_bcwhole, grad_ingain, grad_convvalue, grad_convbc, grad_head, grad_outgain = lax.psum(
        (
            grad_bcspread,
            grad_ingain_spread,
            grad_convvalue_spread,
            grad_convbc_spread,
            grad_head_spread,
            grad_outgain_spread,
        ),
        ("seq", "head"),
    )
    grad_bc = lax.dynamic_slice_in_dim(grad_bcwhole, seq_index * row_count, row_count, 0)
    next_gate = MOMENTUM_KEEP * m_gate + grad_gate
    next_value = MOMENTUM_KEEP * m_value + grad_value
    next_bc = MOMENTUM_KEEP * m_bc + grad_bc
    next_step = MOMENTUM_KEEP * m_step + grad_step
    next_out = MOMENTUM_KEEP * m_out + grad_out
    next_ingain = MOMENTUM_KEEP * m_ingain + grad_ingain
    next_convvalue = MOMENTUM_KEEP * m_convvalue + grad_convvalue
    next_convbc = MOMENTUM_KEEP * m_convbc + grad_convbc
    next_head = MOMENTUM_KEEP * m_head + grad_head
    next_outgain = MOMENTUM_KEEP * m_outgain + grad_outgain
    current = (next_gate.T, next_value.T, next_bc.T, next_step.T, next_out)
    for iteration in range(SWEEPS):
        grams = lax.psum(
            (
                gramian(current[0]),
                gramian(current[1]),
                gramian(current[2]),
                gramian(current[3]),
                gramian(current[4]),
            ),
            "seq",
        )
        if iteration == 0:
            factors = tuple((1.0 / (jnp.sqrt(jnp.trace(member)) + 1e-07) for member in grams))
            current = tuple((member * factor for member, factor in zip(current, factors)))
            grams = tuple((member * factor * factor for member, factor in zip(grams, factors)))
        current = tuple(
            (
                QUINTIC_A * member
                + jnp.dot(
                    QUINTIC_B * square + QUINTIC_C * jnp.dot(square, square, precision=HIGHEST),
                    member,
                    precision=HIGHEST,
                )
                for member, square in zip(current, grams)
            )
        )
    update_gate = current[0].T
    update_value = current[1].T
    update_bc = current[2].T
    update_step = current[3].T
    update_out = current[4]
    update_scale = MATRIX_RATE * MUON_SCALE * math.sqrt(D)
    new_gate = gate_proj - update_scale * update_gate
    new_value = value_proj - update_scale * update_value
    new_bc = bc_proj - update_scale * update_bc
    new_step = step_proj - update_scale * update_step
    new_out = out_proj - update_scale * update_out
    new_ingain = in_gain - VECTOR_RATE * next_ingain
    new_convvalue = conv_value - VECTOR_RATE * next_convvalue
    new_convbc = conv_bc - VECTOR_RATE * next_convbc
    new_head = head_params - VECTOR_RATE * next_head
    new_outgain = out_gain - VECTOR_RATE * next_outgain
    return (
        block_output,
        input_grad,
        grad_gate,
        grad_value,
        grad_bc,
        grad_step,
        grad_out,
        grad_ingain,
        grad_convvalue,
        grad_convbc,
        grad_head,
        grad_outgain,
        new_gate,
        new_value,
        new_bc,
        new_step,
        new_out,
        new_ingain,
        new_convvalue,
        new_convbc,
        new_head,
        new_outgain,
        next_gate,
        next_value,
        next_bc,
        next_step,
        next_out,
        next_ingain,
        next_convvalue,
        next_convbc,
        next_head,
        next_outgain,
    )


def solution(mesh):
    in_specs = (
        P(None, "seq", None),
        P(None, "seq", None),
        P("seq", "head"),
        P("seq", "head"),
        P("seq", None),
        P("seq", "head"),
        P("head", "seq"),
        P(),
        P(),
        P(),
        P(),
        P(),
        P("seq", "head"),
        P("seq", "head"),
        P("seq", None),
        P("seq", "head"),
        P("head", "seq"),
        P(),
        P(),
        P(),
        P(),
        P(),
    )
    out_specs = (
        P(None, "seq", "head"),
        P(None, "seq", "head"),
        P("seq", "head"),
        P("seq", "head"),
        P("seq", None),
        P("seq", "head"),
        P("head", "seq"),
        P(),
        P(),
        P(),
        P(),
        P(),
        P("seq", "head"),
        P("seq", "head"),
        P("seq", None),
        P("seq", "head"),
        P("head", "seq"),
        P(),
        P(),
        P(),
        P(),
        P(),
        P("seq", "head"),
        P("seq", "head"),
        P("seq", None),
        P("seq", "head"),
        P("head", "seq"),
        P(),
        P(),
        P(),
        P(),
        P(),
    )
    return jax.shard_map(
        on_device, mesh=mesh, in_specs=in_specs, out_specs=out_specs, check_vma=False
    )
```

profile of v0, /device:TPU:0, one launch (start us, length us, event | category | flops | bytes accessed | tf_op | source)
XLA Modules:
  0.0 2592.5 jit_solution(613288876843671619)
XLA Ops:
  8.8 32.8 %all-gather.3 = f32[8,192,12]{1,2,0:T(8,128)S(1)} all-gather(f32[1,192,12]{1,2,0:T(8,128)} %bitcast.580), channel_id=1, replica_groups=mesh['seq'=8,'head'=4] {'seq'}, dimensions={0}, use_global_device_ids=true | all-gather | bytes 82944 | tf_op jit(solution)/shard_map/all_gather | solution.py:190
  49.8 7.5 all-gather.13.cloned.1.call-done
  60.0 77.3 %all-gather.11.cloned.1.call-done = f32[1536,768]{1,0:T(8,128)} async-done(((f32[192,768]{1,0:T(8,128)}), f32[1536,768]{1,0:T(8,128)}) %all-gather.11.cloned.1.call-update) | async-done | bytes 4718608 | tf_op jit(solution)/shard_map/all_gather | solution.py:188
  137.3 6.5 fusion.105
  152.0 5.8 all_gather.38
  175.8 20.2 all-gather
  200.4 5.7 fusion.120
  208.4 14.2 all-gather.19.cloned.1.call-done
  226.9 75.9 %all-gather.15.cloned.1.call-done = f32[1536,768]{1,0:T(8,128)} async-done(((f32[192,768]{1,0:T(8,128)}), f32[1536,768]{1,0:T(8,128)}) %all-gather.15.cloned.1.call-update) | async-done | bytes 4718608 | tf_op jit(solution)/shard_map/all_gather | solution.py:187
  302.8 8.2 multiply_reduce_fusion.12
  311.0 5.6 all-reduce.7
  317.3 65.2 %all-gather.17.cloned.1.call-done = f32[768,1536]{0,1:T(8,128)} async-done(((f32[768,192]{0,1:T(8,128)}), f32[768,1536]{0,1:T(8,128)}) %all-gather.17.cloned.1.call-update) | async-done | bytes 4718608 | tf_op jit(solution)/shard_map/all_gather | solution.py:191
  382.5 8.5 multiply_reduce_fusion.8
  391.0 5.6 psum.224
  412.1 7.4 fusion.71
  423.3 42.1 %all-gather.21.cloned.1.call-done = f32[96,64,128]{2,1,0:T(8,128)} async-done(((f32[12,64,128]{2,1,0:T(8,128)}), f32[96,64,128]{2,1,0:T(8,128)}) %all-gather.21.cloned.1.call-update) | async-done | bytes 3145744 | tf_op jit(solution)/shard_map/all_gather | solution.py:38
  466.3 18.5 while.27
  492.5 5.5 fusion.114
  500.4 21.6 all-reduce.27.cloned.1.call-done
  528.5 4.0 collective-permute-done.1
  537.4 5.0 dynamic_update_slice.18
  545.5 5.7 fusion.83
  551.8 7.7 fusion.73
  559.6 5.7 fusion.81
  565.4 109.8 %all-reduce.25.cloned.1.call-done = f32[1536,256]{1,0:T(8,128)} async-done(((f32[1536,256]{1,0:T(8,128)}), f32[1536,256]{1,0:T(8,128)}) %all-reduce.25.cloned.1.call-update) | async-done | bytes 1572880 | tf_op jit(solution)/shard_map/psum | solution.py:321
  678.2 95.8 %reduce-scatter.15.cloned.1.call-done = f32[192,768]{1,0:T(8,128)} async-done(((f32[1536,768]{1,0:T(8,128)}), f32[192,768]{1,0:T(8,128)}) %reduce-scatter.15.cloned.1.call-update) | async-done | bytes 589840 | tf_op jit(solution)/shard_map/reduce_scatter | solution.py:316
  775.2 98.3 %reduce-scatter.19.cloned.1.call-done = f32[768,192]{0,1:T(8,128)} async-done(((f32[768,1536]{0,1:T(8,128)}), f32[768,192]{0,1:T(8,128)}) %reduce-scatter.19.cloned.1.call-update) | async-done | bytes 589840 | tf_op jit(solution)/shard_map/reduce_scatter | solution.py:319
  881.9 91.1 %reduce-scatter.17.cloned.1.call-done = f32[192,768]{1,0:T(8,128)} async-done(((f32[1536,768]{1,0:T(8,128)}), f32[192,768]{1,0:T(8,128)}) %reduce-scatter.17.cloned.1.call-update) | async-done | bytes 589840 | tf_op jit(solution)/shard_map/reduce_scatter | solution.py:317
  978.1 239.9 %all-reduce.39.cloned.1.call-done = (f32[768,768]{1,0:T(8,128)}, f32[768,768]{1,0:T(8,128)}, f32[256,256]{1,0:T(8,128)}, f32[768,768]{1,0:T(8,128)}) async-done(((f32[768,768]{1,0:T(8,128)}, f32[768,768]{1,0:T(8,128)}, f32[256,256]{1,0:T(8,128)}, f32[768,768]{1,0:T(8,128)}), (f32[768,768]{1,0:T(8,128)}, f32[768,768]{1,0:T(8,128)}, f32[256,256]{1,0:T(8,128)}, ...) | async-done | bytes 7340048 | tf_op jit(solution)/shard_map/psum | solution.py:345
  1221.2 8.6 fusion.67
  1229.8 3.8 bitcast_add_fusion.10
  1239.5 8.9 fusion.68
  1248.4 3.8 bitcast_add_fusion.5
  1260.8 9.1 fusion.69
  1276.6 239.0 %all-reduce.37.cloned.1.call-done = (f32[768,768]{1,0:T(8,128)}, f32[768,768]{1,0:T(8,128)}, f32[256,256]{1,0:T(8,128)}, f32[768,768]{1,0:T(8,128)}) async-done(((f32[768,768]{1,0:T(8,128)}, f32[768,768]{1,0:T(8,128)}, f32[256,256]{1,0:T(8,128)}, f32[768,768]{1,0:T(8,128)}), (f32[768,768]{1,0:T(8,128)}, f32[768,768]{1,0:T(8,128)}, f32[256,256]{1,0:T(8,128)}, ...) | async-done | bytes 7340048 | tf_op jit(solution)/shard_map/psum | solution.py:345
  1515.6 8.5 fusion.404
  1531.3 6.2 fusion.411
  1548.2 6.4 fusion.426
  1561.9 7.6 convolution_bitcast_fusion
  1576.1 7.9 fusion.401
  1592.8 6.3 convolution_add_fusion.2
  1604.3 196.8 %all-reduce.35.cloned.1.call-done = (f32[768,768]{1,0:T(8,128)}, f32[768,768]{1,0:T(8,128)}, f32[256,256]{1,0:T(8,128)}, f32[768,768]{1,0:T(8,128)}) async-done(((f32[768,768]{1,0:T(8,128)}, f32[768,768]{1,0:T(8,128)}, f32[256,256]{1,0:T(8,128)}, f32[768,768]{1,0:T(8,128)}), (f32[768,768]{1,0:T(8,128)}, f32[768,768]{1,0:T(8,128)}, f32[256,256]{1,0:T(8,128)}, ...) | async-done | bytes 7340048 | tf_op jit(solution)/shard_map/psum | solution.py:345
  1801.1 8.5 fusion.406
  1819.1 6.4 fusion.413
  1831.8 6.2 fusion.428
  1850.8 4.5 fusion.77
  1872.8 7.5 all-reduce.9
  1886.8 218.7 %all-reduce.33.cloned.1.call-done = (f32[768,768]{1,0:T(8,128)}, f32[768,768]{1,0:T(8,128)}, f32[256,256]{1,0:T(8,128)}, f32[768,768]{1,0:T(8,128)}) async-done(((f32[768,768]{1,0:T(8,128)}, f32[768,768]{1,0:T(8,128)}, f32[256,256]{1,0:T(8,128)}, f32[768,768]{1,0:T(8,128)}), (f32[768,768]{1,0:T(8,128)}, f32[768,768]{1,0:T(8,128)}, f32[256,256]{1,0:T(8,128)}, ...) | async-done | bytes 7340048 | tf_op jit(solution)/shard_map/psum | solution.py:345
  2105.5 8.5 fusion.407
  2120.5 6.4 fusion.414
  2134.2 6.2 fusion.430
  2149.1 21.6 reduce-scatter.21.cloned.1.call-done
  2171.8 19.6 psum.246
  2193.2 17.4 psum.247
  2211.0 19.5 psum.248
  2230.9 17.4 psum.249
  2248.7 19.6 psum.250
  2269.2 35.4 %all-reduce.29.cloned.1.call-done = (f32[1536]{0:T(1024)}, f32[5,3072]{1,0:T(8,128)}, f32[5,256]{1,0:T(8,128)}, f32[3,48]{1,0:T(4,128)}, f32[3072]{0:T(1024)}) async-done(((f32[1536]{0:T(1024)}, f32[5,3072]{1,0:T(8,128)}, f32[5,256]{1,0:T(8,128)}, f32[3,48]{1,0:T(4,128)}, f32[3072]{0:T(1024)}), (f32[1536]{0:T(1024)}, f32[5,3072]{1,0:T(8,128)}, f32[5,256]{1,0:T(8,128)}, f32[3,48]{1,0:T(4,128)}, ...) | async-done | bytes 85584 | tf_op jit(solution)/shard_map/psum | solution.py:321
  2311.4 237.0 %all-reduce.31.cloned.1.call-done = (f32[768,768]{1,0:T(8,128)}, f32[768,768]{1,0:T(8,128)}, f32[256,256]{1,0:T(8,128)}, f32[768,768]{1,0:T(8,128)}) async-done(((f32[768,768]{1,0:T(8,128)}, f32[768,768]{1,0:T(8,128)}, f32[256,256]{1,0:T(8,128)}, f32[768,768]{1,0:T(8,128)}), (f32[768,768]{1,0:T(8,128)}, f32[768,768]{1,0:T(8,128)}, f32[256,256]{1,0:T(8,128)}, ...) | async-done | bytes 7340048 | tf_op jit(solution)/shard_map/psum | solution.py:345
  2548.3 8.5 fusion.408
  2556.9 6.0 fusion.415
  2563.3 6.2 fusion.432
  2573.3 3.8 fusion.150
  2577.2 3.8 fusion.153
  (559 shorter events, 291.3 us)
Async XLA Ops:
  7.2 38.0 %copy-start = (f32[1,256,1536]{2,1,0:T(8,128)S(1)}, f32[1,256,1536]{2,1,0:T(8,128)}, u32[]{:S(2)}) copy-start(f32[1,256,1536]{2,1,0:T(8,128)} %param.26) | copy-start | bytes 4718596
  7.2 38.0 %copy-start.92 = (f32[1536]{0:T(1024)S(1)}, f32[1536]{0:T(1024)}, u32[]{:S(2)}) copy-start(f32[1536]{0:T(1024)} %param.33) | copy-start | bytes 18436
  7.2 50.0 %all-gather.13.cloned.1.call-start = ((), (), s32[]{:S(2)}) async-start(), calls=%async_computation.7 | async-start | bytes 1769472 | tf_op jit(solution)/shard_map/all_gather | solution.py:189
  8.0 129.3 %all-gather.11.cloned.1.call-start = ((), (), s32[]{:S(2)}) async-start(), calls=%async_computation.6 | async-start | bytes 5308416 | tf_op jit(solution)/shard_map/all_gather | solution.py:188
  8.7 213.9 %all-gather.19.cloned.1.call-start = ((), (), s32[]{:S(2)}) async-start(), calls=%async_computation.16 | async-start | bytes 3538944 | tf_op jit(solution)/shard_map/all_gather | solution.py:38
  46.7 97.1 %copy-start.84 = (f32[256,12]{1,0:T(8,128)}, f32[256,12]{1,0:T(8,128)S(1)}, u32[]{:S(2)}) copy-start(f32[256,12]{1,0:T(8,128)S(1)} %fusion.212) | copy-start | bytes 36868
  47.2 96.7 %copy-start.83 = (f32[12,256]{0,1:T(8,128)}, f32[12,256]{0,1:T(8,128)S(1)}, u32[]{:S(2)}) copy-start(f32[12,256]{0,1:T(8,128)S(1)} %copy.204) | copy-start | bytes 36868
  49.0 94.9 %copy-start.145 = (f32[12]{0:T(128)}, f32[12]{0:T(128)S(1)}, u32[]{:S(2)}) copy-start(f32[12]{0:T(128)S(1)} %get-tuple-element.329) | copy-start | bytes 148
  59.9 87.9 %copy-start.67 = (f32[1,256,64]{2,1,0:T(8,128)}, f32[1,256,64]{2,1,0:T(8,128)S(1)}, u32[]{:S(2)}) copy-start(f32[1,256,64]{2,1,0:T(8,128)S(1)} %fusion.206) | copy-start | bytes 196612
  60.0 86.4 %copy-start.128 = (f32[5,256]{1,0:T(8,128)S(1)}, f32[5,256]{1,0:T(8,128)}, u32[]{:S(2)}) copy-start(f32[5,256]{1,0:T(8,128)} %param.35) | copy-start | bytes 15364
  143.9 3.9 collective-permute-start
  146.5 13.2 copy-start.106
  149.3 10.4 copy-start.149
  151.9 48.4 %copy-start.24 = (f32[1,256,768]{1,2,0:T(8,128)}, f32[1,256,768]{1,2,0:T(8,128)S(1)}, u32[]{:S(2)}) copy-start(f32[1,256,768]{1,2,0:T(8,128)S(1)} %copy.197) | copy-start | bytes 2359300
  159.7 9.9 copy-start.69
  161.4 141.4 %all-gather.15.cloned.1.call-start = ((), (), s32[]{:S(2)}) async-start(), calls=%async_computation.8 | async-start | bytes 5308416 | tf_op jit(solution)/shard_map/all_gather | solution.py:187
  162.0 220.5 %all-gather.17.cloned.1.call-start = ((), (), s32[]{:S(2)}) async-start(), calls=%async_computation.9 | async-start | bytes 5308416 | tf_op jit(solution)/shard_map/all_gather | solution.py:191
  162.6 302.9 %all-gather.21.cloned.1.call-start = ((), (), s32[]{:S(2)}) async-start(), calls=%async_computation.17 | async-start | bytes 3538944 | tf_op jit(solution)/shard_map/all_gather | solution.py:38
  196.1 10.0 copy-start.111
  197.1 25.6 copy-start.54
  317.3 79.4 %copy-start.137 = (f32[1,256,1]{1,2,0:T(1,128)}, f32[1,256,1]{1,2,0:T(1,128)S(1)}, u32[]{:S(2)}) copy-start(f32[1,256,1]{1,2,0:T(1,128)S(1)} %get-tuple-element.307) | copy-start | bytes 3076
  317.3 234.5 %copy-start.113 = (f32[1,256,1]{1,2,0:T(1,128)}, f32[1,256,1]{1,2,0:T(1,128)S(1)}, u32[]{:S(2)}) copy-start(f32[1,256,1]{1,2,0:T(1,128)S(1)} %get-tuple-element.308) | copy-start | bytes 3076
  406.6 115.3 %all-reduce.27.cloned.1.call-start = ((), (), s32[]{:S(2)}) async-start(), calls=%async_computation.19 | async-start | bytes 524288
  412.1 9.3 copy-start.57
  492.3 182.9 %all-reduce.25.cloned.1.call-start = ((), (), s32[]{:S(2)}) async-start(), calls=%async_computation.14 | async-start | bytes 3145728 | tf_op jit(solution)/shard_map/psum | solution.py:321
  492.5 31.0 %copy-start.68 = (f32[1,256,64]{2,1,0:T(8,128)S(1)}, f32[1,256,64]{2,1,0:T(8,128)}, u32[]{:S(2)}) copy-start(f32[1,256,64]{2,1,0:T(8,128)} %copy-done.67) | copy-start | bytes 196612
  526.9 5.6 collective-permute-start.1
  532.6 27.0 %copy-start.47 = (f32[1,256,832]{2,1,0:T(8,128)}, f32[1,256,832]{2,1,0:T(8,128)S(1)}, u32[]{:S(2)}) copy-start(f32[1,256,832]{2,1,0:T(8,128)S(1)} %slice_add_fusion) | copy-start | bytes 2555908
  542.5 231.5 %reduce-scatter.15.cloned.1.call-start = ((), (), s32[]{:S(2)}) async-start(), calls=%async_computation.12 | async-start | bytes 5308416 | tf_op jit(solution)/shard_map/reduce_scatter | solution.py:316
  551.3 322.1 %reduce-scatter.19.cloned.1.call-start = ((), (), s32[]{:S(2)}) async-start(), calls=%async_computation.15 | async-start | bytes 5308416 | tf_op jit(solution)/shard_map/reduce_scatter | solution.py:319
  559.5 413.5 %reduce-scatter.17.cloned.1.call-start = ((), (), s32[]{:S(2)}) async-start(), calls=%async_computation.13 | async-start | bytes 5308416 | tf_op jit(solution)/shard_map/reduce_scatter | solution.py:317
  565.3 109.9 %copy-start.104 = (f32[192,256]{1,0:T(8,128)S(1)}, f32[192,256]{1,0:T(8,128)}, u32[]{:S(2)}) copy-start(f32[192,256]{1,0:T(8,128)} %param.40) | copy-start | bytes 589828
  565.3 208.7 %copy-start.96 = (f32[192,768]{1,0:T(8,128)S(1)}, f32[192,768]{1,0:T(8,128)}, u32[]{:S(2)}) copy-start(f32[192,768]{1,0:T(8,128)} %param.38) | copy-start | bytes 1769476
  565.3 652.7 %all-reduce.39.cloned.1.call-start = ((), (), s32[]{:S(2)}) async-start(), calls=%async_computation.25 | async-start | bytes 14680064 | tf_op jit(solution)/shard_map/psum | solution.py:345
  775.1 454.7 %copy-start.20 = (f32[192,768]{1,0:T(8,128)}, f32[192,768]{1,0:T(8,128)S(1)}, u32[]{:S(2)}) copy-start(f32[192,768]{1,0:T(8,128)S(1)} %multiply_add_fusion.8) | copy-start | bytes 1769476
  974.3 274.1 %copy-start.22 = (f32[192,768]{1,0:T(8,128)}, f32[192,768]{1,0:T(8,128)S(1)}, u32[]{:S(2)}) copy-start(f32[192,768]{1,0:T(8,128)S(1)} %multiply_add_fusion.4) | copy-start | bytes 1769476
  977.9 537.7 %all-reduce.37.cloned.1.call-start = ((), (), s32[]{:S(2)}) async-start(), calls=%async_computation.24 | async-start | bytes 14680064 | tf_op jit(solution)/shard_map/psum | solution.py:345
  1260.7 9.1 copy-start.37
  1260.7 9.1 copy-start.43
  1276.4 524.7 %all-reduce.35.cloned.1.call-start = ((), (), s32[]{:S(2)}) async-start(), calls=%async_computation.23 | async-start | bytes 14680064 | tf_op jit(solution)/shard_map/psum | solution.py:345
  1561.8 320.3 %reduce-scatter.11.cloned.1.call-start = ((), (), s32[]{:S(2)}) async-start(), calls=%async_computation.10 | async-start | bytes 1966080 | tf_op jit(solution)/shard_map/reduce_scatter | solution.py:231
  1569.5 312.6 %reduce-scatter.13.cloned.1.call-start = ((), (), s32[]{:S(2)}) async-start(), calls=%async_computation.11 | async-start | bytes 1966080 | tf_op jit(solution)/shard_map/reduce_scatter | solution.py:291
  1576.1 9.4 copy-start.146
  1576.1 10.8 copy-start.4
  1576.1 12.0 copy-start.3
  1604.0 501.5 %all-reduce.33.cloned.1.call-start = ((), (), s32[]{:S(2)}) async-start(), calls=%async_computation.22 | async-start | bytes 14680064 | tf_op jit(solution)/shard_map/psum | solution.py:345
  1801.1 10.8 copy-start.15
  1845.3 36.8 %copy-start.114 = (f32[1,256,1]{1,2,0:T(1,128)S(1)}, f32[1,256,1]{1,2,0:T(1,128)}, u32[]{:S(2)}) copy-start(f32[1,256,1]{1,2,0:T(1,128)} %copy-done.113) | copy-start | bytes 3076
  1845.3 325.4 %reduce-scatter.21.cloned.1.call-start = ((), (), s32[]{:S(2)}) async-start(), calls=%async_computation.18 | async-start | bytes 884736
  1855.3 449.3 %all-reduce.29.cloned.1.call-start = ((), (), s32[]{:S(2)}) async-start(), calls=%async_computation.20 | async-start | bytes 258048 | tf_op jit(solution)/shard_map/psum | solution.py:321
  1886.6 661.8 %all-reduce.31.cloned.1.call-start = ((), (), s32[]{:S(2)}) async-start(), calls=%async_computation.21 | async-start | bytes 14680064 | tf_op jit(solution)/shard_map/psum | solution.py:345
  2148.9 22.7 copy-start.130
  2148.9 119.5 %copy-start.109 = (f32[192,12]{0,1:T(8,128)S(1)}, f32[192,12]{0,1:T(8,128)}, u32[]{:S(2)}) copy-start(f32[192,12]{0,1:T(8,128)} %param.31) | copy-start | bytes 27652
  2148.9 155.6 %copy-start.143 = (f32[3,48]{1,0:T(4,128)S(1)}, f32[3,48]{1,0:T(4,128)}, u32[]{:S(2)}) copy-start(f32[3,48]{1,0:T(4,128)} %param.36) | copy-start | bytes 1732
  2148.9 155.6 %copy-start.150 = (f32[3,48]{1,0:T(4,128)S(1)}, f32[3,48]{1,0:T(4,128)}, u32[]{:S(2)}) copy-start(f32[3,48]{1,0:T(4,128)} %param.46) | copy-start | bytes 1732
  2148.9 156.9 %copy-start.141 = (f32[1536]{0:T(1024)S(1)}, f32[1536]{0:T(1024)}, u32[]{:S(2)}) copy-start(f32[1536]{0:T(1024)} %param.43) | copy-start | bytes 18436
  2149.0 158.2 %copy-start.129 = (f32[5,256]{1,0:T(8,128)S(1)}, f32[5,256]{1,0:T(8,128)}, u32[]{:S(2)}) copy-start(f32[5,256]{1,0:T(8,128)} %param.35) | copy-start | bytes 15364
  2149.0 158.2 %copy-start.142 = (f32[5,256]{1,0:T(8,128)S(1)}, f32[5,256]{1,0:T(8,128)}, u32[]{:S(2)}) copy-start(f32[5,256]{1,0:T(8,128)} %param.45) | copy-start | bytes 15364
  2149.0 159.5 %copy-start.127 = (f32[3072]{0:T(1024)S(1)}, f32[3072]{0:T(1024)}, u32[]{:S(2)}) copy-start(f32[3072]{0:T(1024)} %param.37) | copy-start | bytes 36868
  2149.0 159.4 %copy-start.136 = (f32[3072]{0:T(1024)S(1)}, f32[3072]{0:T(1024)}, u32[]{:S(2)}) copy-start(f32[3072]{0:T(1024)} %param.47) | copy-start | bytes 36868
  2149.0 160.8 %copy-start.105 = (f32[5,3072]{1,0:T(8,128)S(1)}, f32[5,3072]{1,0:T(8,128)}, u32[]{:S(2)}) copy-start(f32[5,3072]{1,0:T(8,128)} %param.34) | copy-start | bytes 184324
  2149.0 160.7 %copy-start.108 = (f32[5,3072]{1,0:T(8,128)S(1)}, f32[5,3072]{1,0:T(8,128)}, u32[]{:S(2)}) copy-start(f32[5,3072]{1,0:T(8,128)} %param.44) | copy-start | bytes 184324
  2171.7 21.4 copy-start.110
  2171.7 385.1 %copy-start.100 = (f32[192,12]{0,1:T(8,128)}, f32[192,12]{0,1:T(8,128)S(1)}, u32[]{:S(2)}) copy-start(f32[192,12]{0,1:T(8,128)S(1)} %multiply_add_fusion.24) | copy-start | bytes 27652
  (112 other events, 539.4 us)
Sparse Core Ops, SparseCore 0:
  10.2 46.9 all-gather.12
  59.4 77.7 all-gather.10
  161.5 60.9 all-gather.18
  224.6 78.1 all-gather.14
  304.8 77.6 all-gather.16
  406.8 58.6 all-gather.20
  492.4 29.5 all-reduce.26
  542.6 132.4 all-reduce.24
  679.4 94.5 reduce-scatter.14
  778.1 95.3 reduce-scatter.18
  877.6 95.3 reduce-scatter.16
  978.0 239.9 all-reduce.38
  1276.5 239.0 all-reduce.36
  1562.0 239.0 all-reduce.34
  1803.5 26.7 reduce-scatter.10
  1832.7 27.9 reduce-scatter.12
  1865.1 240.3 all-reduce.32
  2108.6 62.0 reduce-scatter.20
  2178.7 125.7 all-reduce.28
  2308.9 239.3 all-reduce.30
where the time goes:
time: 2600 us; the launch traced here: 2590 us
  waiting for transfers between devices  1890 us (73%)
  matrix products  352 us (14%)
  blocking collectives  171 us (7%)
  local copies, waits for them, and re-layouts  88.4 us (3%)
  other arithmetic  59 us (2%)
    psum x5, waiting for transfers between devices, on_device(): lax.psum((gramian(current[0]), gramian(current[1]), gramian(current[2]),...  1130 us
    psum x2, waiting for transfers between devices, on_device(): lax.psum((grad_bcspread, grad_ingain_spread, grad_convvalue_spread, grad_...  145 us
    dot_general x25, matrix products, on_device(): jnp.dot(square, square, precision=HIGHEST)  113 us
    reduce_scatter x1, waiting for transfers between devices, on_device(): lax.psum_scatter(grad_outproj, 'seq', scatter_dimension=1, tiled=True)  98.3 us
    reduce_scatter x1, waiting for transfers between devices, on_device(): lax.psum_scatter(grad_gatefull, 'seq', scatter_dimension=0, tiled=True)  95.8 us
    psum x5, blocking collectives, on_device(): lax.psum((gramian(current[0]), gramian(current[1]), gramian(current[2]),...  93.5 us
    reduce_scatter x1, waiting for transfers between devices, on_device(): lax.psum_scatter(grad_valuefull, 'seq', scatter_dimension=0, tiled=True)  91.1 us
    all_gather x1, waiting for transfers between devices, on_device(): lax.all_gather(value_proj, 'seq', axis=0, tiled=True)  77.3 us
  transfers between devices with their start and end apart: 22, of which 20 were waited for; matrix products, arithmetic and copies ran while one was open for 11% of the time, Pallas kernels for 0%

commit v1 on v0

v1 whole, which is shorter than its diff:
```python
import math

import jax
import jax.numpy as jnp
from jax import lax
from jax.sharding import PartitionSpec as P

D = 1536
DI = 3072
STATE = 128
H = 48
GROUP = 256
CONV = 4
SWEEPS = 5


PRECISE = lax.Precision.HIGH
EPSILON = 1e-05
QUINTIC_A = 3.4445
QUINTIC_B = -4.775
QUINTIC_C = 2.0315
MOMENTUM_KEEP = 0.9
MATRIX_RATE = 0.02
VECTOR_RATE = 0.002
MUON_SCALE = 0.2


LANES = 128


def from_behind(value, axis, steps):
    count = lax.axis_size(axis)
    initial, last = (max(0, -steps), min(count, count - steps))
    return lax.ppermute(value, axis, [(source, source + steps) for source in range(initial, last)])


def silu_grad(pre_value):
    sigmoid_val = jax.nn.sigmoid(pre_value)
    return sigmoid_val * (1.0 + pre_value * (1.0 - sigmoid_val))


def project(activation, weight):
    return jnp.einsum("std,dk->stk", activation, weight, precision=PRECISE)


def back_project(upstream, weight):
    return jnp.einsum("stk,dk->std", upstream, weight, precision=PRECISE)


def weight_grad(activation, upstream):
    return jnp.einsum("std,stk->dk", activation, upstream, precision=PRECISE)


def place_slice(portion, full_size, offset, along):
    full_shape = list(portion.shape)
    full_shape[along] = full_size
    return lax.dynamic_update_slice_in_dim(
        jnp.zeros(full_shape, jnp.float32), portion, offset, along
    )


def running_decay(log_decay):
    seq_count, tokens, head_count = log_decay.shape
    blocks = tokens // GROUP
    grouped = log_decay.reshape(seq_count, blocks, GROUP, head_count)
    rows_at = lax.broadcasted_iota(jnp.int32, (GROUP, GROUP), 0)
    cols_at = lax.broadcasted_iota(jnp.int32, (GROUP, GROUP), 1)
    lower_mask = rows_at >= cols_at
    within = jnp.einsum("ij,sbjh->sbih", lower_mask.astype(jnp.float32), grouped, precision=PRECISE)
    group_total = within[:, :, -1, :]
    through = jnp.cumsum(group_total, axis=1)
    before = through - group_total
    return (lower_mask, within, group_total, through, before)


def group_core(values, step_size, log_decay, b_state, c_state, skip_gain):
    seq_count, tokens, width = values.shape
    head_count = step_size.shape[2]
    head_dim = width // head_count
    blocks = tokens // GROUP
    lower_mask, within, group_total, through, before = running_decay(log_decay)
    head_values = values.reshape(seq_count, blocks, GROUP, head_count, head_dim)
    step_blocks = step_size.reshape(seq_count, blocks, GROUP, head_count)
    b_blocks = b_state.reshape(seq_count, blocks, GROUP, -1)
    c_blocks = c_state.reshape(seq_count, blocks, GROUP, -1)
    decay_rows = within.transpose(0, 1, 3, 2)
    log_gaps = decay_rows[..., :, None] - decay_rows[..., None, :]
    decay_mat = jnp.where(lower_mask, jnp.exp(jnp.where(lower_mask, log_gaps, 0.0)), 0.0)
    scores = jnp.einsum("sbin,sbjn->sbij", c_blocks, b_blocks, precision=PRECISE)
    weighted = scores[:, :, None] * decay_mat * step_blocks.transpose(0, 1, 3, 2)[:, :, :, None, :]
    intra_out = jnp.einsum("sbhij,sbjhp->sbihp", weighted, head_values, precision=PRECISE)
    to_end = jnp.exp(group_total[:, :, None, :] - within) * step_blocks
    states = jnp.einsum("sbjh,sbjhp,sbjn->sbhpn", to_end, head_values, b_blocks, precision=PRECISE)
    later_at = lax.broadcasted_iota(jnp.int32, (blocks, blocks), 0)
    earlier_at = lax.broadcasted_iota(jnp.int32, (blocks, blocks), 1)
    earlier_mask = (later_at > earlier_at)[None, :, :, None]
    carry_gap = before[:, :, None, :] - through[:, None, :, :]
    carry_factor = jnp.where(earlier_mask, jnp.exp(jnp.where(earlier_mask, carry_gap, 0.0)), 0.0)
    entering = jnp.einsum("skmh,smhpn->skhpn", carry_factor, states, precision=PRECISE)
    inter_out = (
        jnp.einsum("sbin,sbhpn->sbihp", c_blocks, entering, precision=PRECISE)
        * jnp.exp(within)[..., None]
    )
    output = intra_out + inter_out + skip_gain[:, None] * head_values
    end_gap = through - through
    summary = jnp.einsum("sbh,sbhpn->shpn", jnp.exp(end_gap), states, precision=PRECISE)
    decay_all = jnp.exp(through[:, -1, :])
    return (output.reshape(seq_count, tokens, width), decay_all, summary)


def entry_term(entry_state, log_decay, c_state):
    seq_count, tokens, head_count = log_decay.shape
    blocks = tokens // GROUP
    _, within, _, _, before = running_decay(log_decay)
    reach = jnp.exp(within + before[:, :, None, :])
    c_blocks = c_state.reshape(seq_count, blocks, GROUP, -1)
    result = (
        jnp.einsum("sbin,shpn->sbihp", c_blocks, entry_state, precision=PRECISE) * reach[..., None]
    )
    return result.reshape(seq_count, tokens, -1)


def full_mixer(values, step_size, log_decay, b_state, c_state, skip_gain, entry_state):
    base_out, decay_all, summary = group_core(
        values, step_size, log_decay, b_state, c_state, skip_gain
    )
    output = base_out + entry_term(entry_state, log_decay, c_state)
    leaving = decay_all[..., None, None] * entry_state + summary
    return (output, leaving)


def gather_states(states, totals, axis):
    heads, dims, width = states.shape
    rows = states.reshape(heads * dims, width)
    if totals is not None:
        extra = jnp.pad(totals[None, :], ((0, 7), (0, width - heads)))
        rows = jnp.concatenate([rows, extra], axis=0)
    gathered = lax.all_gather(rows, axis)
    states = gathered[:, : heads * dims].reshape(-1, heads, dims, width)
    return states, None if totals is None else gathered[:, heads * dims, :heads]


def carried_states(gathered, totals, axis, reverse):
    count = lax.axis_size(axis)
    place = lax.axis_index(axis)
    at = jnp.arange(count)
    source, middle = at[:, None], at[None, :]
    if reverse:
        between = (middle > place) & (middle < source)
        used = at > place
    else:
        between = (middle < place) & (middle > source)
        used = at < place
    gap = jnp.sum(jnp.where(between[:, :, None], totals[None, :, :], 0.0), axis=1)
    factor = jnp.where(used[:, None], jnp.exp(gap), 0.0)
    return jnp.sum(factor[:, :, None, None] * gathered, axis=0)


def pack_symmetric(square):
    size = square.shape[0]
    blocks = size // LANES
    packed = []
    for first in range(blocks // 2):
        last = blocks - 1 - first
        packed.append(
            jnp.concatenate(
                [
                    square[row * LANES : (row + 1) * LANES, row * LANES :]
                    for row in (first, last)
                ],
                axis=1,
            )
        )
    return jnp.concatenate(packed, axis=0)


def unpack_symmetric(packed, size):
    blocks = size // LANES
    rows = [None] * blocks
    for first in range(blocks // 2):
        last = blocks - 1 - first
        both = packed[first * LANES : (first + 1) * LANES]
        cut = size - first * LANES
        rows[first] = jnp.pad(both[:, :cut], ((0, 0), (first * LANES, 0)))
        rows[last] = jnp.pad(both[:, cut:], ((0, 0), (last * LANES, 0)))
    upper = jnp.concatenate(rows, axis=0)
    row_block = lax.broadcasted_iota(jnp.int32, (size, size), 0) // LANES
    col_block = lax.broadcasted_iota(jnp.int32, (size, size), 1) // LANES
    return jnp.where(row_block <= col_block, upper, upper.T)


def mult(left, right):
    return jnp.dot(left, right, precision=PRECISE)


def gramian(rows):
    return jnp.einsum("ri,rj->ij", rows, rows, precision=PRECISE)


def orthogonal_rows(rows, gram):
    factor = 1.0 / (jnp.sqrt(jnp.trace(gram)) + 1e-07)
    rows = rows * factor
    gram = gram * (factor * factor)
    for sweep in range(SWEEPS):
        poly = QUINTIC_B * gram + QUINTIC_C * mult(gram, gram)
        rows = QUINTIC_A * rows + mult(rows, poly)
        if sweep < SWEEPS - 1:
            half = QUINTIC_A * gram + mult(poly, gram)
            gram = QUINTIC_A * half + mult(half, poly)
    return rows


def on_device(
    block_input,
    cotangent,
    gate_proj,
    value_proj,
    bc_proj,
    step_proj,
    out_proj,
    in_gain,
    conv_value,
    conv_bc,
    head_params,
    out_gain,
    m_gate,
    m_value,
    m_bc,
    m_step,
    m_out,
    m_ingain,
    m_convvalue,
    m_convbc,
    m_head,
    m_outgain,
):
    head_count = lax.axis_size("head")
    head_index = lax.axis_index("head")
    seq_count, tokens, _ = block_input.shape
    row_count = gate_proj.shape[0]
    inner_width = gate_proj.shape[1]
    local_heads = step_proj.shape[1]
    bc_width = 2 * STATE // head_count
    model_part = D // head_count
    side_width = -(-(bc_width + local_heads) // LANES) * LANES
    bc_cols_mine = lax.dynamic_slice_in_dim(bc_proj, head_index * bc_width, bc_width, 1)
    side_mine = jnp.concatenate(
        [
            value_proj,
            bc_cols_mine,
            step_proj,
            jnp.zeros((row_count, side_width - bc_width - local_heads), jnp.float32),
        ],
        axis=1,
    )
    mixed_full = lax.all_gather(side_mine, "seq", axis=0, tiled=True)
    gate_full = lax.all_gather(gate_proj, "seq", axis=0, tiled=True)
    out_full = lax.all_gather(out_proj.T, "seq", axis=0, tiled=True)
    conv_mine = lax.dynamic_slice_in_dim(conv_value, head_index * inner_width, inner_width, 1)
    gain_mine = lax.dynamic_slice_in_dim(out_gain, head_index * inner_width, inner_width, 0)
    head_mine = lax.dynamic_slice_in_dim(head_params, head_index * local_heads, local_heads, 1)
    bc_taps = lax.dynamic_slice_in_dim(conv_bc, head_index * bc_width, bc_width, 1)
    inv_rms = lax.rsqrt(jnp.mean(block_input * block_input, axis=-1, keepdims=True) + EPSILON)
    normed = block_input * inv_rms * in_gain
    all_pre = project(normed, mixed_full)
    mixed_width = inner_width + bc_width
    mixed_pre = all_pre[..., :mixed_width]
    step_pre = all_pre[..., mixed_width : mixed_width + local_heads]
    gate_pre = project(normed, gate_full)
    conv_taps = jnp.concatenate([conv_mine, bc_taps], axis=-1)
    edge_rows = from_behind(mixed_pre[:, tokens - (CONV - 1) :, :], "seq", 1)
    padded = jnp.concatenate([edge_rows, mixed_pre], axis=1)
    conv_out = conv_taps[CONV] + sum(
        (conv_taps[offset] * padded[:, offset : offset + tokens, :] for offset in range(CONV))
    )
    activated = jax.nn.silu(conv_out)
    values = activated[..., :inner_width]
    bc_all = lax.all_gather(activated[..., inner_width:], "head", axis=2, tiled=True)
    b_state = bc_all[..., :STATE]
    c_state = bc_all[..., STATE:]
    decay_rate = jnp.exp(head_mine[0])
    skip_gain = head_mine[1]
    step_arg = step_pre + head_mine[2]
    step_size = jax.nn.softplus(step_arg)
    log_decay = -decay_rate * step_size
    base_out, _, summary = group_core(values, step_size, log_decay, b_state, c_state, skip_gain)
    states, totals = gather_states(summary[0], jnp.sum(log_decay, axis=(0, 1)), "seq")
    entry_state = carried_states(states, totals, "seq", False)[None]
    mixer_out = base_out + entry_term(entry_state, log_decay, c_state)
    gate_act = jax.nn.silu(gate_pre)
    gated = mixer_out * gate_act
    square_part = jnp.sum(gated * gated, axis=-1, keepdims=True)
    out_part = back_project(gated * gain_mine, out_full)
    out_sum = lax.psum_scatter(out_part, "head", scatter_dimension=2, tiled=True)
    square_sum = lax.psum(square_part, "head")
    gate_rms = lax.rsqrt(square_sum / DI + EPSILON)
    input_mine = lax.dynamic_slice_in_dim(block_input, head_index * model_part, model_part, 2)
    cotangent_mine = lax.dynamic_slice_in_dim(cotangent, head_index * model_part, model_part, 2)
    block_output = input_mine + gate_rms * out_sum
    normed_out = gated * gate_rms * gain_mine
    grad_outfull = weight_grad(cotangent, normed_out)
    grad_normout = project(cotangent, out_full)
    grad_outgain_mine = jnp.sum(grad_normout * gated * gate_rms, axis=(0, 1))
    scaled = grad_normout * gain_mine
    dot_total = lax.psum(jnp.sum(scaled * gated, axis=-1, keepdims=True), "head")
    grad_gated = gate_rms * scaled - gate_rms**3 * gated * dot_total / DI
    grad_mixer = grad_gated * gate_act
    grad_gate_pre = grad_gated * mixer_out * silu_grad(gate_pre)
    grad_gatefull = weight_grad(normed, grad_gate_pre)
    _, entry_back = jax.vjp(lambda entering: entry_term(entering, log_decay, c_state), entry_state)
    direct = entry_back(grad_mixer)[0]
    directs, _ = gather_states(direct[0], None, "seq")
    leave_grad = carried_states(directs, totals, "seq", True)[None]
    _, mixer_back = jax.vjp(
        full_mixer, values, step_size, log_decay, b_state, c_state, skip_gain, entry_state
    )
    grad_values, grad_stepsize, grad_logdecay, grad_b, grad_c, grad_skip, _ = mixer_back(
        (grad_mixer, leave_grad)
    )
    grad_step_total = grad_stepsize - grad_logdecay * decay_rate
    grad_alog = jnp.sum(grad_logdecay * log_decay, axis=(0, 1))
    grad_step_pre = grad_step_total * jax.nn.sigmoid(step_arg)
    grad_bias = jnp.sum(grad_step_pre, axis=(0, 1))
    grad_bc_all = jnp.concatenate([grad_b, grad_c], axis=-1)
    grad_bc_act = lax.psum_scatter(grad_bc_all, "head", scatter_dimension=2, tiled=True)
    grad_conv = jnp.concatenate([grad_values, grad_bc_act], axis=-1) * silu_grad(conv_out)
    grad_taps = jnp.stack(
        [
            jnp.sum(grad_conv * padded[:, offset : offset + tokens, :], axis=(0, 1))
            for offset in range(CONV)
        ]
        + [jnp.sum(grad_conv, axis=(0, 1))]
    )
    grad_padded = sum(
        (
            jnp.pad(conv_taps[offset] * grad_conv, ((0, 0), (offset, CONV - 1 - offset), (0, 0)))
            for offset in range(CONV)
        )
    )
    edge_back = from_behind(grad_padded[:, : CONV - 1, :], "seq", -1)
    grad_mixed = grad_padded[:, CONV - 1 :, :] + jnp.pad(
        edge_back, ((0, 0), (tokens - (CONV - 1), 0), (0, 0))
    )
    grad_all_pre = jnp.concatenate(
        [
            grad_mixed,
            grad_step_pre,
            jnp.zeros((seq_count, tokens, side_width - bc_width - local_heads), jnp.float32),
        ],
        axis=-1,
    )
    grad_mixedfull = weight_grad(normed, grad_all_pre)
    grad_normed = back_project(grad_gate_pre, gate_full) + back_project(grad_all_pre, mixed_full)
    stat_part = jnp.sum(grad_normed * in_gain * block_input, axis=-1, keepdims=True)
    normed_grad_mine = lax.psum_scatter(grad_normed, "head", scatter_dimension=2, tiled=True)
    stat_total = lax.psum(stat_part, "head")
    gain_part = lax.dynamic_slice_in_dim(in_gain, head_index * model_part, model_part, 0)
    input_grad = (
        cotangent_mine
        + inv_rms * gain_part * normed_grad_mine
        - inv_rms**3 * input_mine * stat_total / D
    )
    grad_ingain_mine = jnp.sum(normed_grad_mine * input_mine * inv_rms, axis=(0, 1))
    grad_out_rows = lax.psum_scatter(grad_outfull, "seq", scatter_dimension=0, tiled=True)
    grad_gate = lax.psum_scatter(grad_gatefull, "seq", scatter_dimension=0, tiled=True)
    grad_mixed_rows = lax.psum_scatter(grad_mixedfull, "seq", scatter_dimension=0, tiled=True)
    grad_value = grad_mixed_rows[:, :inner_width]
    grad_bc = lax.all_gather(
        grad_mixed_rows[:, inner_width:mixed_width], "head", axis=1, tiled=True
    )
    grad_step = grad_mixed_rows[:, mixed_width : mixed_width + local_heads]
    grad_out = grad_out_rows.T
    next_out_rows = MOMENTUM_KEEP * m_out.T + grad_out_rows
    next_gate = MOMENTUM_KEEP * m_gate + grad_gate
    next_value = MOMENTUM_KEEP * m_value + grad_value
    next_bc = MOMENTUM_KEEP * m_bc + grad_bc
    next_step = MOMENTUM_KEEP * m_step + grad_step
    next_out = MOMENTUM_KEEP * m_out + grad_out
    pieces = (
        grad_ingain_mine,
        grad_taps.reshape(-1),
        grad_alog,
        grad_skip,
        grad_bias,
        grad_outgain_mine,
    )
    flat = jnp.concatenate(pieces)
    flat_rows = -(-flat.shape[0] // (8 * LANES)) * 8
    flat = jnp.pad(flat, (0, flat_rows * LANES - flat.shape[0])).reshape(flat_rows, LANES)
    side = 2 * STATE
    small_gram = jnp.pad(gramian(next_step), ((0, -local_heads % 8), (0, side - local_heads)))
    out_gram = lax.psum(pack_symmetric(gramian(next_out_rows)), "seq")
    gate_gram = lax.psum(pack_symmetric(gramian(next_gate)), "seq")
    value_gram, side_gram, flat = lax.psum(
        (
            pack_symmetric(gramian(next_value)),
            jnp.concatenate([gramian(next_bc), small_gram], axis=0),
            flat,
        ),
        "seq",
    )
    flat = lax.all_gather(flat, "head").reshape(head_count, flat_rows * LANES)
    parts = []
    start = 0
    for piece in pieces:
        parts.append(flat[:, start : start + piece.shape[0]])
        start += piece.shape[0]
    grad_ingain = parts[0].reshape(D)
    taps_all = parts[1].reshape(head_count, CONV + 1, mixed_width)
    grad_convvalue = taps_all[:, :, :inner_width].transpose(1, 0, 2).reshape(CONV + 1, DI)
    grad_convbc = taps_all[:, :, inner_width:].transpose(1, 0, 2).reshape(CONV + 1, 2 * STATE)
    grad_head = jnp.stack([parts[2].reshape(H), parts[3].reshape(H), parts[4].reshape(H)])
    grad_outgain = parts[5].reshape(DI)
    next_ingain = MOMENTUM_KEEP * m_ingain + grad_ingain
    next_convvalue = MOMENTUM_KEEP * m_convvalue + grad_convvalue
    next_convbc = MOMENTUM_KEEP * m_convbc + grad_convbc
    next_head = MOMENTUM_KEEP * m_head + grad_head
    next_outgain = MOMENTUM_KEEP * m_outgain + grad_outgain
    update_out = orthogonal_rows(next_out_rows, unpack_symmetric(out_gram, inner_width)).T
    update_gate = orthogonal_rows(next_gate, unpack_symmetric(gate_gram, inner_width))
    update_value = orthogonal_rows(next_value, unpack_symmetric(value_gram, inner_width))
    update_bc = orthogonal_rows(next_bc, side_gram[:side])
    update_step = orthogonal_rows(next_step, side_gram[side : side + local_heads, :local_heads])
    update_scale = MATRIX_RATE * MUON_SCALE * math.sqrt(D)
    new_gate = gate_proj - update_scale * update_gate
    new_value = value_proj - update_scale * update_value
    new_bc = bc_proj - update_scale * update_bc
    new_step = step_proj - update_scale * update_step
    new_out = out_proj - update_scale * update_out
    new_ingain = in_gain - VECTOR_RATE * next_ingain
    new_convvalue = conv_value - VECTOR_RATE * next_convvalue
    new_convbc = conv_bc - VECTOR_RATE * next_convbc
    new_head = head_params - VECTOR_RATE * next_head
    new_outgain = out_gain - VECTOR_RATE * next_outgain
    return (
        block_output,
        input_grad,
        grad_gate,
        grad_value,
        grad_bc,
        grad_step,
        grad_out,
        grad_ingain,
        grad_convvalue,
        grad_convbc,
        grad_head,
        grad_outgain,
        new_gate,
        new_value,
        new_bc,
        new_step,
        new_out,
        new_ingain,
        new_convvalue,
        new_convbc,
        new_head,
        new_outgain,
        next_gate,
        next_value,
        next_bc,
        next_step,
        next_out,
        next_ingain,
        next_convvalue,
        next_convbc,
        next_head,
        next_outgain,
    )


def solution(mesh):
    in_specs = (
        P(None, "seq", None),
        P(None, "seq", None),
        P("seq", "head"),
        P("seq", "head"),
        P("seq", None),
        P("seq", "head"),
        P("head", "seq"),
        P(),
        P(),
        P(),
        P(),
        P(),
        P("seq", "head"),
        P("seq", "head"),
        P("seq", None),
        P("seq", "head"),
        P("head", "seq"),
        P(),
        P(),
        P(),
        P(),
        P(),
    )
    out_specs = (
        P(None, "seq", "head"),
        P(None, "seq", "head"),
        P("seq", "head"),
        P("seq", "head"),
        P("seq", None),
        P("seq", "head"),
        P("head", "seq"),
        P(),
        P(),
        P(),
        P(),
        P(),
        P("seq", "head"),
        P("seq", "head"),
        P("seq", None),
        P("seq", "head"),
        P("head", "seq"),
        P(),
        P(),
        P(),
        P(),
        P(),
        P("seq", "head"),
        P("seq", "head"),
        P("seq", None),
        P("seq", "head"),
        P("head", "seq"),
        P(),
        P(),
        P(),
        P(),
        P(),
    )
    return jax.shard_map(
        on_device, mesh=mesh, in_specs=in_specs, out_specs=out_specs, check_vma=False
    )
```

time: 2600 us -> 1260 us (0.48)
  waiting for transfers between devices: 1890 us -> 735 us
  blocking collectives: 171 us -> 75 us
  matrix products: 352 us -> 276 us
    psum x7 -> x1, waiting for transfers between devices: 1280 us -> 110 us  [on_device(): gate_gram = lax.psum(pack_symmetric(gramian(next_gate)), 'seq')]
    reduce_scatter x3 -> x2, waiting for transfers between devices: 285 us -> 201 us  [the longest x1 105 us: on_device(): lax.psum_scatter(grad_mixedfull, 'seq', scatter_dimension=0, tiled=True)]
    dot_general x101 -> x114, matrix products: 337 us -> 254 us  [the longest x90 176 us: mult(): return jnp.dot(left, right, precision=PRECISE)]
    all_gather x6 -> x5, waiting for transfers between devices: 282 us -> 331 us  [the longest x2 100 us: gather_states(): gathered = lax.all_gather(rows, axis)]
    psum x5 -> x3, blocking collectives: 93.5 us -> 51.9 us  [the longest x1 39 us: on_device(): lax.psum((pack_symmetric(gramian(next_value)), jnp.concatenate([gramian(n...]
    all_gather x2, blocking collectives: 53 us -> 11.5 us  [the longest x1 6.23 us: on_device(): lax.all_gather(grad_mixed_rows[:, inner_width:mixed_width], 'head', axis=...]
  transfers between devices with their start and end apart: 22 -> 14, of which waited for: 20 -> 12; matrix products, arithmetic and copies ran while one was open for 11% -> 12% of each run, Pallas kernels for 0% -> 0%
where the time goes in v1:
time: 1260 us; the launch traced here: 1250 us
  waiting for transfers between devices  735 us (58%)
  matrix products  276 us (22%)
  blocking collectives  75 us (6%)
  local copies, waits for them, and re-layouts  74.5 us (6%)
  other arithmetic  65.8 us (5%)
  between operations  21 us (2%)
    dot_general x90, matrix products, mult(): return jnp.dot(left, right, precision=PRECISE)  176 us
    psum x1, waiting for transfers between devices, on_device(): gate_gram = lax.psum(pack_symmetric(gramian(next_gate)), 'seq')  110 us
    reduce_scatter x1, waiting for transfers between devices, on_device(): lax.psum_scatter(grad_mixedfull, 'seq', scatter_dimension=0, tiled=True)  105 us
    all_gather x2, waiting for transfers between devices, gather_states(): gathered = lax.all_gather(rows, axis)  100 us
    reduce_scatter x1, waiting for transfers between devices, on_device(): lax.psum_scatter(grad_outfull, 'seq', scatter_dimension=0, tiled=True)  95.5 us
    all_gather x1, waiting for transfers between devices, on_device(): mixed_full = lax.all_gather(side_mine, 'seq', axis=0, tiled=True)  89.6 us
    all_gather x1, waiting for transfers between devices, on_device(): gate_full = lax.all_gather(gate_proj, 'seq', axis=0, tiled=True)  75 us
    all_gather x1, waiting for transfers between devices, on_device(): out_full = lax.all_gather(out_proj.T, 'seq', axis=0, tiled=True)  66.5 us
  transfers between devices with their start and end apart: 14, of which 12 were waited for; matrix products, arithmetic and copies ran while one was open for 12% of the time, Pallas kernels for 0%

profile of v1, /device:TPU:0, one launch (start us, length us, event | category | flops | bytes accessed | tf_op | source)
XLA Modules:
  0.0 1253.2 jit_solution(717026180101001072)
XLA Ops:
  13.7 89.6 %all-gather.8.cloned.1.call-done = f32[1536,896]{1,0:T(8,128)} async-done(((f32[192,896]{1,0:T(8,128)}), f32[1536,896]{1,0:T(8,128)}) %all-gather.8.cloned.1.call-update) | async-done | bytes 5505040 | tf_op jit(solution)/shard_map/all_gather | solution.py:256
  103.3 7.1 fusion.133
  116.2 6.2 collective-permute-done
  125.0 5.8 all_gather.31
  138.2 4.0 fusion.148
  142.2 54.1 %all-gather.14.cloned.1.call-done = f32[6208,128]{1,0:T(8,128)} async-done(((f32[776,128]{1,0:T(8,128)}), f32[6208,128]{1,0:T(8,128)}) %all-gather.14.cloned.1.call-update) | async-done | bytes 3178512 | tf_op jit(solution)/shard_map/all_gather | solution.py:138
  201.5 75.0 %all-gather.10.cloned.1.call-done = f32[1536,768]{1,0:T(8,128)} async-done(((f32[192,768]{1,0:T(8,128)}), f32[1536,768]{1,0:T(8,128)}) %all-gather.10.cloned.1.call-update) | async-done | bytes 4718608 | tf_op jit(solution)/shard_map/all_gather | solution.py:257
  276.5 7.6 multiply_reduce_fusion.13
  284.1 5.6 psum.56
  289.7 66.5 %all-gather.12.cloned.1.call-done = f32[1536,768]{1,0:T(8,128)} async-done(((f32[192,768]{1,0:T(8,128)}), f32[1536,768]{1,0:T(8,128)}) %all-gather.12.cloned.1.call-update) | async-done | bytes 4718608 | tf_op jit(solution)/shard_map/all_gather | solution.py:258
  356.2 8.2 multiply_reduce_fusion.9
  364.4 5.8 psum.57
  379.5 5.7 fusion.108
  389.0 46.0 %all-gather.16.cloned.1.call-done = f32[6144,128]{1,0:T(8,128)} async-done(((f32[768,128]{1,0:T(8,128)}), f32[6144,128]{1,0:T(8,128)}) %all-gather.16.cloned.1.call-update) | async-done | bytes 3145744 | tf_op jit(solution)/shard_map/all_gather | solution.py:138
  440.2 7.3 fusion.115
  448.2 5.6 convolution_bitcast_fusion
  453.8 6.1 copy.866
  472.6 4.5 fusion.142
  478.0 5.1 fusion.487
  486.3 13.5 %collective-permute-done.1 = f32[1,3,832]{1,2,0:T(8,128)S(1)} collective-permute-done((f32[1,3,832]{1,2,0:T(8,128)S(1)}, f32[1,3,832]{1,2,0:T(8,128)S(1)}, u32[]{:S(2)}, u32[]{:S(2)}) %collective-permute-start.1) | collective-permute-done | bytes 10016 | tf_op jit(solution)/shard_map/ppermute | solution.py:34
  500.3 7.3 fusion.113
  507.8 7.6 convolution_bitcast_fusion.1
  515.5 6.5 fusion.494
  522.0 9.1 fusion.109
  531.4 47.5 %reduce-scatter.16.cloned.1.call-done = f32[192,768]{1,0:T(8,128)} async-done(((f32[1536,768]{1,0:T(8,128)}), f32[192,768]{1,0:T(8,128)}) %reduce-scatter.16.cloned.1.call-update) | async-done | bytes 589840
  582.9 95.5 %reduce-scatter.20.cloned.1.call-done = f32[192,768]{1,0:T(8,128)} async-done(((f32[1536,768]{1,0:T(8,128)}), f32[192,768]{1,0:T(8,128)}) %reduce-scatter.20.cloned.1.call-update) | async-done | bytes 589840 | tf_op jit(solution)/shard_map/reduce_scatter | solution.py:364
  683.6 105.1 %reduce-scatter.18.cloned.1.call-done = f32[192,896]{1,0:T(8,128)} async-done(((f32[1536,896]{1,0:T(8,128)}), f32[192,896]{1,0:T(8,128)}) %reduce-scatter.18.cloned.1.call-update) | async-done | bytes 688144 | tf_op jit(solution)/shard_map/reduce_scatter | solution.py:366
  796.4 6.2 all_gather.37
  817.4 7.2 psum.58
  824.6 24.5 %reduce-scatter.14.cloned.1.call-done = f32[1,256,384]{2,1,0:T(8,128)} async-done(((f32[1,256,1536]{2,1,0:T(8,128)}), f32[1,256,384]{2,1,0:T(8,128)}) %reduce-scatter.14.cloned.1.call-update) | async-done | bytes 393232 | tf_op jit(solution)/shard_map/reduce_scatter | solution.py:355
  851.5 39.0 %psum.59 = f32[1,48,128]{2,1,0:T(8,128)S(1)} all-reduce(f32[1,48,128]{2,1,0:T(8,128)S(1)} %pad_bitcast_fusion), channel_id=1, replica_groups=mesh['seq'=8,'head'=4] {'seq'}, use_global_device_ids=true, to_apply=%region_39.40 | all-reduce | flops 6144 | bytes 49152 | tf_op jit(solution)/shard_map/psum | solution.py:394
  890.6 5.3 all_gather.39
  905.5 110.3 %all-reduce.32.cloned.1.call-done = (f32[384,896]{0,1:T(8,128)}, f32[384,896]{1,0:T(8,128)}, f32[272,256]{1,0:T(8,128)}, f32[384,896]{1,0:T(8,128)}) async-done(((f32[384,896]{0,1:T(8,128)}, f32[384,896]{1,0:T(8,128)}, f32[272,256]{1,0:T(8,128)}, f32[384,896]{1,0:T(8,128)}), (f32[384,896]{0,1:T(8,128)}, f32[384,896]{1,0:T(8,128)}, f32[272,256]{1,0:T(8,128)}, ...) | async-done | bytes 4407312 | tf_op jit(solution)/shard_map/psum | solution.py:393
  1054.3 8.9 select_reduce_fusion
  1063.9 5.5 fusion.104
  1071.8 4.7 multiply_add_fusion.67
  1077.2 5.5 fusion.99
  1085.2 4.7 multiply_add_fusion.43
  1094.6 7.0 multiply_add_fusion.66
  1104.6 3.4 multiply_add_fusion.61
  1109.5 3.2 multiply_add_fusion.60
  1115.7 3.6 multiply_add_fusion.55
  1120.7 3.2 multiply_add_fusion.54
  1126.9 3.3 multiply_add_fusion.49
  1131.7 3.2 multiply_add_fusion.48
  1135.0 4.4 fusion.500
  1139.4 3.2 multiply_add_fusion.42
  1142.6 3.2 fusion.502
  1150.5 3.2 multiply_add_fusion.36
  1153.7 3.4 fusion.503
  1157.1 3.2 multiply_add_fusion.31
  1161.8 3.2 multiply_add_fusion.30
  1168.0 3.3 multiply_add_fusion.25
  1173.6 3.2 multiply_add_fusion.24
  1176.8 4.4 fusion.505
  1191.8 3.2 multiply_add_fusion.19
  1195.1 3.2 multiply_add_fusion.18
  1198.3 3.4 fusion.508
  1208.0 3.4 multiply_add_fusion.12
  1214.3 3.2 multiply_add_fusion.7
  1219.0 3.2 multiply_add_fusion.6
  1222.2 3.2 fusion.510
  1230.0 3.2 multiply_add_fusion
  1233.3 3.2 fusion.511
  (515 shorter events, 211.5 us)
Async XLA Ops:
  7.2 96.1 %copy-start.63 = (f32[1536]{0:T(1024)S(1)}, f32[1536]{0:T(1024)}, u32[]{:S(2)}) copy-start(f32[1536]{0:T(1024)} %param.29) | copy-start | bytes 18436
  7.2 96.1 %all-gather.8.cloned.1.call-start = ((), (), s32[]{:S(2)}) async-start(), calls=%async_computation.5 | async-start | bytes 6193152 | tf_op jit(solution)/shard_map/all_gather | solution.py:256
  11.4 184.9 %all-gather.14.cloned.1.call-start = ((), (), s32[]{:S(2)}) async-start(), calls=%async_computation.10 | async-start | bytes 3575808 | tf_op jit(solution)/shard_map/all_gather | solution.py:138
  12.3 110.0 %copy-start.84 = (f32[832]{0:T(1024)}, f32[832]{0:T(1024)S(1)}, u32[]{:S(2)}) copy-start(f32[832]{0:T(1024)S(1)} %get-tuple-element.305) | copy-start | bytes 9988
  12.3 110.0 %copy-start.86 = (f32[832]{0:T(1024)}, f32[832]{0:T(1024)S(1)}, u32[]{:S(2)}) copy-start(f32[832]{0:T(1024)S(1)} %get-tuple-element.306) | copy-start | bytes 9988
  12.3 110.0 %copy-start.88 = (f32[832]{0:T(1024)}, f32[832]{0:T(1024)S(1)}, u32[]{:S(2)}) copy-start(f32[832]{0:T(1024)S(1)} %get-tuple-element.307) | copy-start | bytes 9988
  12.3 110.0 %copy-start.90 = (f32[832]{0:T(1024)}, f32[832]{0:T(1024)S(1)}, u32[]{:S(2)}) copy-start(f32[832]{0:T(1024)S(1)} %get-tuple-element.308) | copy-start | bytes 9988
  12.6 98.0 %copy-start.113 = (f32[12]{0:T(128)}, f32[12]{0:T(128)S(1)}, u32[]{:S(2)}) copy-start(f32[12]{0:T(128)S(1)} %fusion.485) | copy-start | bytes 148
  13.2 97.2 %copy-start.79 = (f32[256]{0:T(256)}, f32[256]{0:T(256)S(1)}, u32[]{:S(2)}) copy-start(f32[256]{0:T(256)S(1)} %get-tuple-element.378) | copy-start | bytes 3076
  13.7 101.1 %copy-start.106 = (f32[12]{0:T(128)}, f32[12]{0:T(128)S(1)}, u32[]{:S(2)}) copy-start(f32[12]{0:T(128)S(1)} %get-tuple-element.376) | copy-start | bytes 148
  110.4 14.4 %copy-start.12 = (f32[1,256,896]{1,2,0:T(8,128)}, f32[1,256,896]{1,2,0:T(8,128)S(1)}, u32[]{:S(2)}) copy-start(f32[1,256,896]{1,2,0:T(8,128)S(1)} %fusion.133) | copy-start | bytes 2752516
  110.6 11.7 copy-start.71
  112.3 12.4 copy-start.107
  112.4 12.4 copy-start.109
  112.4 10.0 collective-permute-start
  116.2 8.8 copy-start.19
  124.8 6.0 copy-start.20
  124.8 7.5 copy-start.112
  131.1 255.5 %copy-start.37 = (f32[1,256,128]{2,1,0:T(8,128)}, f32[1,256,128]{2,1,0:T(8,128)S(1)}, u32[]{:S(2)}) copy-start(f32[1,256,128]{2,1,0:T(8,128)S(1)} %copy.869) | copy-start | bytes 393220
  132.3 9.9 copy-start.31
  133.2 143.3 %all-gather.10.cloned.1.call-start = ((), (), s32[]{:S(2)}) async-start(), calls=%async_computation.6 | async-start | bytes 5308416 | tf_op jit(solution)/shard_map/all_gather | solution.py:257
  133.9 222.3 %all-gather.12.cloned.1.call-start = ((), (), s32[]{:S(2)}) async-start(), calls=%async_computation.7 | async-start | bytes 5308416 | tf_op jit(solution)/shard_map/all_gather | solution.py:258
  134.5 300.4 %all-gather.16.cloned.1.call-start = ((), (), s32[]{:S(2)}) async-start(), calls=%async_computation.11 | async-start | bytes 3538944 | tf_op jit(solution)/shard_map/all_gather | solution.py:138
  135.9 6.3 copy-start.77
  142.2 57.6 %copy-start.64 = (f32[256,12]{0,1:T(8,128)S(1)}, f32[256,12]{0,1:T(8,128)}, u32[]{:S(2)}) copy-start(f32[256,12]{0,1:T(8,128)} %get-tuple-element.368) | copy-start | bytes 36868
  197.4 79.1 %copy-start.80 = (f32[256]{0:T(256)S(1)}, f32[256]{0:T(256)}, u32[]{:S(2)}) copy-start(f32[256]{0:T(256)} %copy-done.79) | copy-start | bytes 3076
  199.8 76.7 %copy-start.27 = (f32[768,128]{1,0:T(8,128)}, f32[768,128]{1,0:T(8,128)S(1)}, u32[]{:S(2)}) copy-start(f32[768,128]{1,0:T(8,128)S(1)} %fusion) | copy-start | bytes 1179652
  289.7 80.5 %copy-start.92 = (f32[1,256,1]{1,2,0:T(1,128)}, f32[1,256,1]{1,2,0:T(1,128)S(1)}, u32[]{:S(2)}) copy-start(f32[1,256,1]{1,2,0:T(1,128)S(1)} %get-tuple-element.344) | copy-start | bytes 3076
  289.7 80.5 %copy-start.102 = (f32[1,256,1]{1,2,0:T(1,128)}, f32[1,256,1]{1,2,0:T(1,128)S(1)}, u32[]{:S(2)}) copy-start(f32[1,256,1]{1,2,0:T(1,128)S(1)} %get-tuple-element.343) | copy-start | bytes 3076
  376.1 101.0 %all-reduce.30.cloned.1.call-start = ((), (), s32[]{:S(2)}) async-start(), calls=%async_computation.15 | async-start | bytes 524288
  379.5 6.0 copy-start.21
  379.5 6.0 copy-start.32
  379.5 6.6 copy-start.28
  379.5 6.5 copy-start.41
  387.6 47.4 %copy-start.73 = (f32[8,768]{1,0:T(8,128)S(1)}, f32[8,768]{1,0:T(8,128)}, u32[]{:S(2)}) copy-start(f32[8,768]{1,0:T(8,128)} %mul.1173) | copy-start | bytes 73732
  440.0 138.9 %reduce-scatter.16.cloned.1.call-start = ((), (), s32[]{:S(2)}) async-start(), calls=%async_computation.12 | async-start | bytes 5308416
  447.5 230.9 %reduce-scatter.20.cloned.1.call-start = ((), (), s32[]{:S(2)}) async-start(), calls=%async_computation.14 | async-start | bytes 5308416 | tf_op jit(solution)/shard_map/reduce_scatter | solution.py:364
  460.0 6.5 copy-start.29
  460.0 328.7 %reduce-scatter.18.cloned.1.call-start = ((), (), s32[]{:S(2)}) async-start(), calls=%async_computation.13 | async-start | bytes 6193152 | tf_op jit(solution)/shard_map/reduce_scatter | solution.py:366
  484.0 16.3 %copy-start.81 = (f32[256]{0:T(256)S(1)}, f32[256]{0:T(256)}, u32[]{:S(2)}) copy-start(f32[256]{0:T(256)} %copy-done.79) | copy-start | bytes 3076
  484.0 15.9 %collective-permute-start.1 = (f32[1,3,832]{1,2,0:T(8,128)S(1)}, f32[1,3,832]{1,2,0:T(8,128)S(1)}, u32[]{:S(2)}, u32[]{:S(2)}) collective-permute-start(f32[1,3,832]{1,2,0:T(8,128)S(1)} %pad_add_fusion.1), channel_id=1, source_target_pairs={{4,0},{8,4},{12,8},{16,12},{20,16},{24,20},{28,24},{5,1},{9,5},{13... | collective-permute-start | bytes 29960 | tf_op jit(solution)/shard_map/ppermute | solution.py:34
  507.6 317.0 %reduce-scatter.12.cloned.1.call-start = ((), (), s32[]{:S(2)}) async-start(), calls=%async_computation.8 | async-start | bytes 1966080 | tf_op jit(solution)/shard_map/reduce_scatter | solution.py:294
  515.5 333.6 %reduce-scatter.14.cloned.1.call-start = ((), (), s32[]{:S(2)}) async-start(), calls=%async_computation.9 | async-start | bytes 1966080 | tf_op jit(solution)/shard_map/reduce_scatter | solution.py:355
  522.0 56.9 %copy-start.59 = (f32[192,768]{1,0:T(8,128)S(1)}, f32[192,768]{1,0:T(8,128)}, u32[]{:S(2)}) copy-start(f32[192,768]{1,0:T(8,128)} %param.34) | copy-start | bytes 1769476
  531.1 484.6 %all-reduce.32.cloned.1.call-start = ((), (), s32[]{:S(2)}) async-start(), calls=%async_computation.16 | async-start | bytes 8814592 | tf_op jit(solution)/shard_map/psum | solution.py:393
  580.1 489.4 %copy-start.14 = (f32[192,768]{1,0:T(8,128)}, f32[192,768]{1,0:T(8,128)S(1)}, u32[]{:S(2)}) copy-start(f32[192,768]{1,0:T(8,128)S(1)} %multiply_add_fusion.145) | copy-start | bytes 1769476
  580.1 98.4 %copy-start.33 = (f32[768,192]{0,1:T(8,128)S(1)}, f32[768,192]{0,1:T(8,128)}, u32[]{:S(2)}) copy-start(f32[768,192]{0,1:T(8,128)} %param.38) | copy-start | bytes 1769476
  790.8 291.9 %copy-start.17 = (f32[192,768]{1,0:T(8,128)}, f32[192,768]{1,0:T(8,128)S(1)}, u32[]{:S(2)}) copy-start(f32[192,768]{1,0:T(8,128)S(1)} %get-tuple-element.336) | copy-start | bytes 1769476
  792.1 13.4 %copy-start.99 = (f32[192,12]{0,1:T(8,128)S(1)}, f32[192,12]{0,1:T(8,128)}, u32[]{:S(2)}) copy-start(f32[192,12]{0,1:T(8,128)} %param.37) | copy-start | bytes 27652
  811.6 37.5 %copy-start.82 = (f32[256]{0:T(256)S(1)}, f32[256]{0:T(256)}, u32[]{:S(2)}) copy-start(f32[256]{0:T(256)} %copy-done.79) | copy-start | bytes 3076
  811.7 39.8 %copy-start.98 = (f32[768]{0:T(1024)S(1)}, f32[768]{0:T(1024)}, u32[]{:S(2)}) copy-start(f32[768]{0:T(1024)} %get-tuple-element.295) | copy-start | bytes 9220
  811.7 39.8 %copy-start.114 = (f32[12]{0:T(128)S(1)}, f32[12]{0:T(128)}, u32[]{:S(2)}) copy-start(f32[12]{0:T(128)} %get-tuple-element.338) | copy-start | bytes 148
  811.7 39.8 %copy-start.115 = (f32[12]{0:T(128)S(1)}, f32[12]{0:T(128)}, u32[]{:S(2)}) copy-start(f32[12]{0:T(128)} %get-tuple-element.352) | copy-start | bytes 148
  896.0 123.7 %copy-start.95 = (f32[1536]{0:T(1024)}, f32[1536]{0:T(1024)S(1)}, u32[]{:S(2)}) copy-start(f32[1536]{0:T(1024)S(1)} %reshape.940) | copy-start | bytes 18436
  896.1 124.5 %copy-start.62 = (f32[4,5,768]{2,1,0:T(8,128)}, f32[4,5,768]{2,1,0:T(8,128)S(1)}, u32[]{:S(2)}) copy-start(f32[4,5,768]{2,1,0:T(8,128)S(1)} %slice.347) | copy-start | bytes 184324
  896.3 124.4 %copy-start.96 = (f32[5,256]{1,0:T(8,128)}, f32[5,256]{1,0:T(8,128)S(1)}, u32[]{:S(2)}) copy-start(f32[5,256]{1,0:T(8,128)S(1)} %reshape.943) | copy-start | bytes 15364
  896.6 124.1 %copy-start.78 = (f32[3072]{0:T(1024)}, f32[3072]{0:T(1024)S(1)}, u32[]{:S(2)}) copy-start(f32[3072]{0:T(1024)S(1)} %reshape.944) | copy-start | bytes 36868
  1015.7 6.7 copy-start.54
  1017.6 9.1 copy-start.53
  1037.2 7.0 copy-start.66
  1069.5 7.0 copy-start.10
  1077.2 5.6 copy-start.1
  1085.2 6.4 copy-start.43
  1085.2 9.1 copy-start.70
  (69 other events, 214.8 us)
Sparse Core Ops, SparseCore 0:
  11.5 91.8 all-gather.7
  133.3 62.8 all-gather.13
  198.5 77.9 all-gather.9
  278.5 77.6 all-gather.11
  376.2 58.6 all-gather.15
  440.1 30.9 all-reduce.29
  475.3 103.5 reduce-scatter.15
  583.1 95.2 reduce-scatter.19
  682.1 106.5 reduce-scatter.17
  791.0 27.3 reduce-scatter.11
  821.0 28.0 reduce-scatter.13
  853.5 162.1 all-reduce.31

commit v2 on v1

--- a/solution.py
+++ b/solution.py
@@ -1,8 +1,11 @@
+import functools
 import math
 
 import jax
 import jax.numpy as jnp
 from jax import lax
+from jax.experimental import pallas as pl
+from jax.experimental.pallas import tpu as pltpu
 from jax.sharding import PartitionSpec as P
 
 D = 1536
@@ -32,6 +35,257 @@
     count = lax.axis_size(axis)
     initial, last = (max(0, -steps), min(count, count - steps))
     return lax.ppermute(value, axis, [(source, source + steps) for source in range(initial, last)])
+
+
+def ring_place(index, count):
+    odd = index % 2
+    return (1 - odd) * (index // 2) + odd * (count - 1 - index // 2)
+
+
+def ring_index(position, count):
+    position = (position + 2 * count) % count
+    back = position // (count // 2)
+    return (1 - back) * (2 * position) + back * (2 * (count - 1 - position) + 1)
+
+
+def greet(axis, neighbours):
+    barrier = pltpu.get_barrier_semaphore()
+    for neighbour in neighbours:
+        pl.semaphore_signal(
+            barrier, inc=1, device_id={axis: neighbour}, device_id_type=pl.DeviceIdType.MESH
+        )
+    pl.semaphore_wait(barrier, len(neighbours))
+
+
+def piece_count(half, arrays):
+    return 2 if arrays == 1 and half % 16 == 0 else 1
+
+
+def relay_step(axis, count, backward, refs):
+    own, decay, near, entering, leaving, send_sem, recv_sem = refs
+    me = lax.axis_index(axis)
+    order = count - 1 - me if backward else me
+    ahead = (me + count - 1) % count if backward else (me + 1) % count
+    copy = pltpu.make_async_remote_copy(
+        src_ref=leaving,
+        dst_ref=entering,
+        send_sem=send_sem,
+        recv_sem=recv_sem,
+        device_id={axis: ahead},
+        device_id_type=pl.DeviceIdType.MESH,
+    )
+
+    def turn(at):
+        @pl.when(order == at)
+        def _():
+            if at:
+                copy.wait_recv()
+                near[...] = entering[...]
+                if at < count - 1:
+                    leaving[...] = own[...] + decay[...] * entering[...]
+            else:
+                near[...] = jnp.zeros_like(near)
+                leaving[...] = own[...]
+            if at < count - 1:
+                copy.start()
+
+    def finish():
+        turn(count - 1)
+
+        @pl.when(order < count - 1)
+        def _():
+            copy.wait_send()
+
+    return turn, finish
+
+
+def relay_parts(relay):
+    if relay is None:
+        return [], [], []
+    state = relay[0]
+    buffers = [pltpu.VMEM(state.shape, state.dtype)] * 2
+    return (
+        [relay[0], relay[1]],
+        [jax.ShapeDtypeStruct(state.shape, state.dtype)],
+        buffers + [pltpu.SemaphoreType.DMA(()), pltpu.SemaphoreType.DMA(())],
+    )
+
+
+def ring_neighbours(axis, count, relayed):
+    me = lax.axis_index(axis)
+    place = ring_place(me, count)
+    right, left = ring_index(place + 1, count), ring_index(place - 1, count)
+    greeted = (left, right)
+    if relayed:
+        greeted += ((me + 1) % count, (me + count - 1) % count)
+    greet(axis, greeted)
+    return me, place, right, left
+
+
+def ring_gather_kernel(axis, count, arrays, backward, *refs):
+    relayed = backward is not None
+    turn, finish = (lambda at: None), (lambda: None)
+    if relayed:
+        states, refs = refs[:2], refs[2:]
+        near, refs = refs[2 * arrays], refs[: 2 * arrays] + refs[2 * arrays + 1 :]
+        turn, finish = relay_step(axis, count, backward, (*states, near, *refs[-4:]))
+        refs = refs[:-4]
+    shards, outs = refs[:arrays], refs[arrays : 2 * arrays]
+    send_sem, recv_sem, own_sem = refs[2 * arrays :]
+    me, place, right, left = ring_neighbours(axis, count, relayed)
+    own = []
+    for j in range(arrays):
+        rows = shards[j].shape[0]
+        start = pl.multiple_of(me * rows, 8)
+        own.append(
+            pltpu.make_async_copy(shards[j], outs[j].at[pl.ds(start, rows)], own_sem.at[j])
+        )
+    flights = {}
+    for step in range(count - 1):
+        for j in range(arrays):
+            rows = shards[j].shape[0]
+            pieces = piece_count(rows // 2, arrays)
+            length = rows // 2 // pieces
+            for piece in range(pieces):
+                for way, sign, target in ((0, -1, right), (1, 1, left)):
+                    origin = ring_index(place + sign * step, count)
+                    within = (way * pieces + piece) * length
+                    region = pl.ds(pl.multiple_of(origin * rows + within, 8), length)
+                    if step:
+                        flights[step - 1, j, piece, way].wait_recv()
+                        source = outs[j].at[region]
+                    else:
+                        source = shards[j].at[pl.ds(within, length)]
+                    flight = pltpu.make_async_remote_copy(
+                        src_ref=source,
+                        dst_ref=outs[j].at[region],
+                        send_sem=send_sem.at[way, j + piece, step],
+                        recv_sem=recv_sem.at[way, j + piece, step],
+                        device_id={axis: target},
+                        device_id_type=pl.DeviceIdType.MESH,
+                    )
+                    flights[step, j, piece, way] = flight
+                    flight.start()
+        if step == 0:
+            for copy in own:
+                copy.start()
+        turn(step)
+    for (step, *_), flight in flights.items():
+        if step == count - 2:
+            flight.wait_recv()
+    finish()
+    for copy in own:
+        copy.wait()
+    for flight in flights.values():
+        flight.wait_send()
+
+
+def busy_cost(sent):
+    return pl.CostEstimate(flops=6000 * sent, bytes_accessed=2 * sent, transcendentals=0)
+
+
+def ring_gather(shards, axis, collective_id, relay=None):
+    count = lax.axis_size(axis)
+    arrays = len(shards)
+    states, near, relay_scratch = relay_parts(relay)
+    backward = None if relay is None else relay[2]
+    sent = sum(shard.size for shard in shards) * 4 * (count - 1)
+    return pl.pallas_call(
+        functools.partial(ring_gather_kernel, axis, count, arrays, backward),
+        out_shape=[
+            jax.ShapeDtypeStruct((count * shard.shape[0], shard.shape[1]), shard.dtype)
+            for shard in shards
+        ]
+        + near,
+        in_specs=[pl.BlockSpec(memory_space=pltpu.VMEM)] * (arrays + len(states)),
+        out_specs=[pl.BlockSpec(memory_space=pl.ANY)] * arrays
+        + [pl.BlockSpec(memory_space=pltpu.VMEM)] * len(near),
+        scratch_shapes=[
+            pltpu.SemaphoreType.DMA((2, max(arrays, 2), count - 1)),
+            pltpu.SemaphoreType.DMA((2, max(arrays, 2), count - 1)),
+            pltpu.SemaphoreType.DMA((arrays,)),
+        ]
+        + relay_scratch,
+        compiler_params=pltpu.CompilerParams(collective_id=collective_id, has_side_effects=True),
+        cost_estimate=busy_cost(sent),
+        name=f"ring_gather_{collective_id}",
+    )(*states, *shards)
+
+
+def ring_scatter_kernel(axis, count, arrays, backward, *refs):
+    relayed = backward is not None
+    turn, finish = (lambda at: None), (lambda: None)
+    if relayed:
+        states, refs = refs[:2], refs[2:]
+        near, refs = refs[2 * arrays], refs[: 2 * arrays] + refs[2 * arrays + 1 :]
+        turn, finish = relay_step(axis, count, backward, (*states, near, *refs[-4:]))
+        refs = refs[:-4]
+    parts, outs, slots = refs[:arrays], refs[arrays : 2 * arrays], refs[2 * arrays : 3 * arrays]
+    send_sem, recv_sem = refs[3 * arrays :]
+    me, place, right, left = ring_neighbours(axis, count, relayed)
+    flights = {}
+    for step in range(count):
+        for j in range(arrays):
+            rows = outs[j].shape[0]
+            pieces = piece_count(rows // 2, arrays)
+            length = rows // 2 // pieces
+            for piece in range(pieces):
+                part = pl.ds(piece * length, length)
+                for way, sign, target in ((0, -1, right), (1, 1, left)):
+                    goal = ring_index(place + sign * (1 + step), count)
+                    within = (way * pieces + piece) * length
+                    region = pl.ds(pl.multiple_of(goal * rows + within, 8), length)
+                    if step:
+                        flights[step - 1, j, piece, way].wait_recv()
+                        total = slots[j][way, step - 1, part, :] + parts[j][region, :]
+                        if step == count - 1:
+                            outs[j][pl.ds(within, length), :] = total
+                            continue
+                        slots[j][way, step - 1, part, :] = total
+                        source = slots[j].at[way, step - 1, part]
+                    else:
+                        source = parts[j].at[region]
+                    flight = pltpu.make_async_remote_copy(
+                        src_ref=source,
+                        dst_ref=slots[j].at[way, step, part],
+                        send_sem=send_sem.at[way, j + piece, step],
+                        recv_sem=recv_sem.at[way, j + piece, step],
+                        device_id={axis: target},
+                        device_id_type=pl.DeviceIdType.MESH,
+                    )
+                    flights[step, j, piece, way] = flight
+                    flight.start()
+        if step < count - 1:
+            turn(step)
+    finish()
+    for flight in flights.values():
+        flight.wait_send()
+
+
+def ring_scatter(parts, axis, collective_id, relay=None):
+    count = lax.axis_size(axis)
+    arrays = len(parts)
+    states, near, relay_scratch = relay_parts(relay)
+    backward = None if relay is None else relay[2]
+    shapes = [(part.shape[0] // count, part.shape[1]) for part in parts]
+    sent = sum(part.size for part in parts) * 4
+    return pl.pallas_call(
+        functools.partial(ring_scatter_kernel, axis, count, arrays, backward),
+        out_shape=[jax.ShapeDtypeStruct(shape, jnp.float32) for shape in shapes] + near,
+        in_specs=[pl.BlockSpec(memory_space=pltpu.VMEM)] * (arrays + len(states)),
+        out_specs=[pl.BlockSpec(memory_space=pltpu.VMEM)] * (arrays + len(near)),
+        scratch_shapes=[
+            pltpu.VMEM((2, count - 1, rows // 2, columns), jnp.float32) for rows, columns in shapes
+        ]
+        + [
+            pltpu.SemaphoreType.DMA((2, max(arrays, 2), count - 1)),
+            pltpu.SemaphoreType.DMA((2, max(arrays, 2), count - 1)),
+        ]
+        + relay_scratch,
+        compiler_params=pltpu.CompilerParams(collective_id=collective_id, has_side_effects=True),
+        cost_estimate=busy_cost(sent),
+        name=f"ring_scatter_{collective_id}",
+    )(*states, *parts)
 
 
 def silu_grad(pre_value):
@@ -129,85 +383,123 @@
     return (output, leaving)
 
 
-def gather_states(states, totals, axis):
-    heads, dims, width = states.shape
-    rows = states.reshape(heads * dims, width)
-    if totals is not None:
-        extra = jnp.pad(totals[None, :], ((0, 7), (0, width - heads)))
-        rows = jnp.concatenate([rows, extra], axis=0)
-    gathered = lax.all_gather(rows, axis)
-    states = gathered[:, : heads * dims].reshape(-1, heads, dims, width)
-    return states, None if totals is None else gathered[:, heads * dims, :heads]
-
-
-def carried_states(gathered, totals, axis, reverse):
-    count = lax.axis_size(axis)
-    place = lax.axis_index(axis)
-    at = jnp.arange(count)
-    source, middle = at[:, None], at[None, :]
-    if reverse:
-        between = (middle > place) & (middle < source)
-        used = at > place
-    else:
-        between = (middle < place) & (middle > source)
-        used = at < place
-    gap = jnp.sum(jnp.where(between[:, :, None], totals[None, :, :], 0.0), axis=1)
-    factor = jnp.where(used[:, None], jnp.exp(gap), 0.0)
-    return jnp.sum(factor[:, :, None, None] * gathered, axis=0)
-
-
-def pack_symmetric(square):
-    size = square.shape[0]
-    blocks = size // LANES
-    packed = []
-    for first in range(blocks // 2):
-        last = blocks - 1 - first
-        packed.append(
-            jnp.concatenate(
-                [
-                    square[row * LANES : (row + 1) * LANES, row * LANES :]
-                    for row in (first, last)
-                ],
-                axis=1,
-            )
-        )
-    return jnp.concatenate(packed, axis=0)
-
-
-def unpack_symmetric(packed, size):
-    blocks = size // LANES
-    rows = [None] * blocks
-    for first in range(blocks // 2):
-        last = blocks - 1 - first
-        both = packed[first * LANES : (first + 1) * LANES]
-        cut = size - first * LANES
-        rows[first] = jnp.pad(both[:, :cut], ((0, 0), (first * LANES, 0)))
-        rows[last] = jnp.pad(both[:, cut:], ((0, 0), (last * LANES, 0)))
-    upper = jnp.concatenate(rows, axis=0)
-    row_block = lax.broadcasted_iota(jnp.int32, (size, size), 0) // LANES
-    col_block = lax.broadcasted_iota(jnp.int32, (size, size), 1) // LANES
-    return jnp.where(row_block <= col_block, upper, upper.T)
-
-
-def mult(left, right):
-    return jnp.dot(left, right, precision=PRECISE)
-
-
-def gramian(rows):
-    return jnp.einsum("ri,rj->ij", rows, rows, precision=PRECISE)
-
-
-def orthogonal_rows(rows, gram):
-    factor = 1.0 / (jnp.sqrt(jnp.trace(gram)) + 1e-07)
-    rows = rows * factor
-    gram = gram * (factor * factor)
-    for sweep in range(SWEEPS):
-        poly = QUINTIC_B * gram + QUINTIC_C * mult(gram, gram)
-        rows = QUINTIC_A * rows + mult(rows, poly)
-        if sweep < SWEEPS - 1:
-            half = QUINTIC_A * gram + mult(poly, gram)
-            gram = QUINTIC_A * half + mult(half, poly)
-    return rows
+def halves(value):
+    high = value.astype(jnp.bfloat16)
+    return high, (value - high.astype(jnp.float32)).astype(jnp.bfloat16)
+
+
+def three_pass(left, right):
+    def one(a, b):
+        return jnp.dot(a, b, preferred_element_type=jnp.float32)
+
+    return one(left[0], right[0]) + (one(left[0], right[1]) + one(left[1], right[0]))
+
+
+def gram_strips(rows):
+    size = rows.shape[1]
+    block = min(size, 256)
+    return [
+        jnp.einsum("ri,rj->ij", rows[:, at : at + block], rows[:, at:], precision=PRECISE)
+        for at in range(0, size, block)
+    ]
+
+
+def orthogonal_kernel(arrays, strip_counts, *refs):
+
+    grams = []
+    for strips in strip_counts:
+        grams.append(refs[:strips])
+        refs = refs[strips:]
+    rows, outs, scratch = refs[:arrays], refs[arrays : 2 * arrays], refs[2 * arrays :]
+    work = [scratch[8 * j : 8 * j + 8] for j in range(arrays)]
+    for j in range(arrays):
+        whole = work[j][0]
+        block = grams[j][0].shape[0]
+        spots = [slice(at * block, (at + 1) * block) for at in range(len(grams[j]))]
+        across = lax.broadcasted_iota(jnp.int32, (block, block), 0)
+        down = lax.broadcasted_iota(jnp.int32, (block, block), 1)
+        total = jnp.zeros((1, 1), jnp.float32)
+        for strip in grams[j]:
+            diagonal = jnp.where(across == down, strip[:, :block], 0.0)
+            total += jnp.sum(jnp.sum(diagonal, axis=0, keepdims=True), axis=1, keepdims=True)
+        factor = 1.0 / (jnp.sqrt(total) + 1e-07)
+        square = factor * factor
+        for i, strip in enumerate(grams[j]):
+            for k in range(i, len(spots)):
+                piece = strip[:, (k - i) * block : (k - i + 1) * block] * square
+                whole[spots[i], spots[k]] = piece
+                if i != k:
+                    whole[spots[k], spots[i]] = piece.T
+        outs[j][...] = rows[j][...] * factor
+
+    def split_whole(j, at):
+        whole, high, low = work[j][0], work[j][1], work[j][2]
+        high[at, :], low[at, :] = halves(whole[at, :])
+
+    def sweep(last):
+        strips = []
+        for j in range(arrays):
+            size = rows[j].shape[1]
+            strip = min(size, 256)
+            strips.append([slice(s, s + strip) for s in range(0, size, strip)])
+        for j in range(arrays):
+            for at in strips[j]:
+                split_whole(j, at)
+        for j in range(arrays):
+            whole, high, low, poly_h, poly_l, _, _, _ = work[j]
+            for at in strips[j]:
+                poly = QUINTIC_B * whole[at, :] + QUINTIC_C * three_pass(
+                    (high[at, :], low[at, :]), (high[...], low[...])
+                )
+                poly_h[at, :], poly_l[at, :] = halves(poly)
+        for j in range(arrays):
+            poly = (work[j][3][...], work[j][4][...])
+            value = outs[j][...]
+            outs[j][...] = QUINTIC_A * value + three_pass(halves(value), poly)
+        if last:
+            return
+        for j in range(arrays):
+            whole, high, low, poly_h, poly_l, half, half_h, half_l = work[j]
+            for at in strips[j]:
+                value = QUINTIC_A * whole[at, :] + three_pass(
+                    (poly_h[at, :], poly_l[at, :]), (high[...], low[...])
+                )
+                half[at, :] = value
+                half_h[at, :], half_l[at, :] = halves(value)
+        for j in range(arrays):
+            whole, _, _, poly_h, poly_l, half, half_h, half_l = work[j]
+            for at in strips[j]:
+                whole[at, :] = QUINTIC_A * half[at, :] + three_pass(
+                    (half_h[at, :], half_l[at, :]), (poly_h[...], poly_l[...])
+                )
+
+    def body(_, carry):
+        sweep(False)
+        return carry
+
+    lax.fori_loop(0, SWEEPS - 1, body, 0)
+    sweep(True)
+
+
+def orthogonal_rows(pairs, name):
+    arrays = len(pairs)
+    scratch = []
+    flops = 0
+    for _, rows in pairs:
+        size = rows.shape[1]
+        full, narrow = pltpu.VMEM((size, size), jnp.float32), pltpu.VMEM((size, size), jnp.bfloat16)
+        scratch += [full, narrow, narrow, narrow, narrow, full, narrow, narrow]
+        flops += 6 * (13 * size**3 + 5 * rows.shape[0] * size**2)
+    return pl.pallas_call(
+        functools.partial(orthogonal_kernel, arrays, [len(strips) for strips, _ in pairs]),
+        out_shape=[jax.ShapeDtypeStruct(rows.shape, jnp.float32) for _, rows in pairs],
+        in_specs=[pl.BlockSpec(memory_space=pltpu.VMEM)]
+        * (arrays + sum(len(strips) for strips, _ in pairs)),
+        out_specs=[pl.BlockSpec(memory_space=pltpu.VMEM)] * arrays,
+        scratch_shapes=scratch,
+        cost_estimate=pl.CostEstimate(flops=flops, bytes_accessed=0, transcendentals=0),
+        name=name,
+    )(*[strip for strips, _ in pairs for strip in strips], *[rows for _, rows in pairs])
 
 
 def on_device(
@@ -253,9 +545,7 @@
         ],
         axis=1,
     )
-    mixed_full = lax.all_gather(side_mine, "seq", axis=0, tiled=True)
-    gate_full = lax.all_gather(gate_proj, "seq", axis=0, tiled=True)
-    out_full = lax.all_gather(out_proj.T, "seq", axis=0, tiled=True)
+    (mixed_full,) = ring_gather((side_mine,), "seq", 0)
     conv_mine = lax.dynamic_slice_in_dim(conv_value, head_index * inner_width, inner_width, 1)
     gain_mine = lax.dynamic_slice_in_dim(out_gain, head_index * inner_width, inner_width, 0)
     head_mine = lax.dynamic_slice_in_dim(head_params, head_index * local_heads, local_heads, 1)
@@ -266,7 +556,6 @@
     mixed_width = inner_width + bc_width
     mixed_pre = all_pre[..., :mixed_width]
     step_pre = all_pre[..., mixed_width : mixed_width + local_heads]
-    gate_pre = project(normed, gate_full)
     conv_taps = jnp.concatenate([conv_mine, bc_taps], axis=-1)
     edge_rows = from_behind(mixed_pre[:, tokens - (CONV - 1) :, :], "seq", 1)
     padded = jnp.concatenate([edge_rows, mixed_pre], axis=1)
@@ -283,9 +572,17 @@
     step_arg = step_pre + head_mine[2]
     step_size = jax.nn.softplus(step_arg)
     log_decay = -decay_rate * step_size
-    base_out, _, summary = group_core(values, step_size, log_decay, b_state, c_state, skip_gain)
-    states, totals = gather_states(summary[0], jnp.sum(log_decay, axis=(0, 1)), "seq")
-    entry_state = carried_states(states, totals, "seq", False)[None]
+    base_out, decay_all, summary = group_core(
+        values, step_size, log_decay, b_state, c_state, skip_gain
+    )
+    state_shape = summary.shape
+    state_rows = (-1, state_shape[-1])
+    decay_rows = jnp.broadcast_to(decay_all[..., None, None], state_shape).reshape(state_rows)
+    gate_full, out_full, entry_rows = ring_gather(
+        (gate_proj, out_proj.T), "seq", 1, (summary.reshape(state_rows), decay_rows, False)
+    )
+    entry_state = entry_rows.reshape(state_shape)
+    gate_pre = project(normed, gate_full)
     mixer_out = base_out + entry_term(entry_state, log_decay, c_state)
     gate_act = jax.nn.silu(gate_pre)
     gated = mixer_out * gate_act
@@ -309,8 +606,10 @@
     grad_gatefull = weight_grad(normed, grad_gate_pre)
     _, entry_back = jax.vjp(lambda entering: entry_term(entering, log_decay, c_state), entry_state)
     direct = entry_back(grad_mixer)[0]
-    directs, _ = gather_states(direct[0], None, "seq")
-    leave_grad = carried_states(directs, totals, "seq", True)[None]
+    grad_out_rows, grad_gate, leave_rows = ring_scatter(
+        (grad_outfull, grad_gatefull), "seq", 2, (direct.reshape(state_rows), decay_rows, True)
+    )
+    leave_grad = leave_rows.reshape(state_shape)
     _, mixer_back = jax.vjp(
         full_mixer, values, step_size, log_decay, b_state, c_state, skip_gain, entry_state
     )
@@ -360,10 +659,8 @@
         + inv_rms * gain_part * normed_grad_mine
         - inv_rms**3 * input_mine * stat_total / D
     )
-    grad_ingain_mine = jnp.sum(normed_grad_mine * input_mine * inv_rms, axis=(0, 1))
-    grad_out_rows = lax.psum_scatter(grad_outfull, "seq", scatter_dimension=0, tiled=True)
-    grad_gate = lax.psum_scatter(grad_gatefull, "seq", scatter_dimension=0, tiled=True)
-    grad_mixed_rows = lax.psum_scatter(grad_mixedfull, "seq", scatter_dimension=0, tiled=True)
+    grad_ingain_part = jnp.sum(grad_normed * block_input * inv_rms, axis=(0, 1))
+    (grad_mixed_rows,) = ring_scatter((grad_mixedfull,), "seq", 3)
     grad_value = grad_mixed_rows[:, :inner_width]
     grad_bc = lax.all_gather(
         grad_mixed_rows[:, inner_width:mixed_width], "head", axis=1, tiled=True
@@ -377,7 +674,7 @@
     next_step = MOMENTUM_KEEP * m_step + grad_step
     next_out = MOMENTUM_KEEP * m_out + grad_out
     pieces = (
-        grad_ingain_mine,
+        grad_ingain_part,
         grad_taps.reshape(-1),
         grad_alog,
         grad_skip,
@@ -385,27 +682,33 @@
         grad_outgain_mine,
     )
     flat = jnp.concatenate(pieces)
-    flat_rows = -(-flat.shape[0] // (8 * LANES)) * 8
-    flat = jnp.pad(flat, (0, flat_rows * LANES - flat.shape[0])).reshape(flat_rows, LANES)
+    flat_rows = -(-flat.shape[0] // (16 * STATE)) * 8
+    flat = jnp.pad(flat, (0, flat_rows * 2 * STATE - flat.shape[0])).reshape(flat_rows, 2 * STATE)
     side = 2 * STATE
-    small_gram = jnp.pad(gramian(next_step), ((0, -local_heads % 8), (0, side - local_heads)))
-    out_gram = lax.psum(pack_symmetric(gramian(next_out_rows)), "seq")
-    gate_gram = lax.psum(pack_symmetric(gramian(next_gate)), "seq")
-    value_gram, side_gram, flat = lax.psum(
-        (
-            pack_symmetric(gramian(next_value)),
-            jnp.concatenate([gramian(next_bc), small_gram], axis=0),
-            flat,
-        ),
+    strips = len(gram_strips(next_gate))
+    early = lax.psum(gram_strips(next_out_rows) + gram_strips(next_gate), "seq")
+    out_gram, gate_gram = early[:strips], early[strips:]
+    late_value, _ = lax.optimization_barrier((next_value, early))
+    (step_gram,) = gram_strips(next_step)
+    step_gram = jnp.pad(step_gram, ((0, -local_heads % 8), (0, side - local_heads)))
+    late = lax.psum(
+        gram_strips(late_value)
+        + [jnp.concatenate(gram_strips(next_bc) + [step_gram, flat], axis=0)],
         "seq",
     )
-    flat = lax.all_gather(flat, "head").reshape(head_count, flat_rows * LANES)
+    value_gram, side_gram = late[:-1], late[-1]
+    flat = side_gram[side + step_gram.shape[0] :]
+    step_gram = jnp.pad(
+        side_gram[side : side + step_gram.shape[0], :LANES],
+        ((0, LANES - step_gram.shape[0]), (0, 0)),
+    )
+    flat = lax.all_gather(flat, "head").reshape(head_count, flat_rows * 2 * STATE)
     parts = []
     start = 0
     for piece in pieces:
         parts.append(flat[:, start : start + piece.shape[0]])
         start += piece.shape[0]
-    grad_ingain = parts[0].reshape(D)
+    grad_ingain = jnp.sum(parts[0], axis=0)
     taps_all = parts[1].reshape(head_count, CONV + 1, mixed_width)
     grad_convvalue = taps_all[:, :, :inner_width].transpose(1, 0, 2).reshape(CONV + 1, DI)
     grad_convbc = taps_all[:, :, inner_width:].transpose(1, 0, 2).reshape(CONV + 1, 2 * STATE)
@@ -416,11 +719,19 @@
     next_convbc = MOMENTUM_KEEP * m_convbc + grad_convbc
     next_head = MOMENTUM_KEEP * m_head + grad_head
     next_outgain = MOMENTUM_KEEP * m_outgain + grad_outgain
-    update_out = orthogonal_rows(next_out_rows, unpack_symmetric(out_gram, inner_width)).T
-    update_gate = orthogonal_rows(next_gate, unpack_symmetric(gate_gram, inner_width))
-    update_value = orthogonal_rows(next_value, unpack_symmetric(value_gram, inner_width))
-    update_bc = orthogonal_rows(next_bc, side_gram[:side])
-    update_step = orthogonal_rows(next_step, side_gram[side : side + local_heads, :local_heads])
+    update_out, update_gate = orthogonal_rows(
+        ((out_gram, next_out_rows), (gate_gram, next_gate)), "ortho_first"
+    )
+    update_out = update_out.T
+    update_value, update_bc, update_step = orthogonal_rows(
+        (
+            (value_gram, next_value),
+            ([side_gram[:side]], next_bc),
+            ([step_gram], jnp.pad(next_step, ((0, 0), (0, LANES - local_heads)))),
+        ),
+        "ortho_last",
+    )
+    update_step = update_step[:, :local_heads]
     update_scale = MATRIX_RATE * MUON_SCALE * math.sqrt(D)
     new_gate = gate_proj - update_scale * update_gate
     new_value = value_proj - update_scale * update_value

time: 1260 us -> 843 us (0.67)
  waiting for transfers between devices: 735 us -> 67.9 us
  Pallas kernels: 0 us -> 530 us
  matrix products: 276 us -> 100 us
  local copies, waits for them, and re-layouts: 74.5 us -> 28.6 us
  blocking collectives: 75 us -> 36.9 us
  other arithmetic: 65.8 us -> 49.3 us
    pallas_call x0 -> x6, Pallas kernels: none -> 530 us  [the longest x2 231 us: ring_scatter(): pl.pallas_call(functools.partial(ring_scatter_kernel, axis, count, arrays...]
    all_gather x5 -> x0, waiting for transfers between devices: 331 us -> none  [the longest x2 100 us: gather_states(): gathered = lax.all_gather(rows, axis)]
    reduce_scatter x2 -> x0, waiting for transfers between devices: 201 us -> none  [the longest x1 105 us: on_device(): lax.psum_scatter(grad_mixedfull, 'seq', scatter_dimension=0, tiled=True)]
    dot_general x95 -> x11, matrix products: 182 us -> 13.1 us  [gram_strips(): jnp.einsum('ri,rj->ij', rows[:, at:at + block], rows[:, at:], precision=P...]
    psum x1 -> x2, waiting for transfers between devices: 110 us -> 54.1 us  [the longest x1 54.1 us: on_device(): lax.psum(gram_strips(late_value) + [jnp.concatenate(gram_strips(next_bc)...]
    unnamed x14 -> x6, waiting for transfers between devices: 48.9 us -> 0.08 us
    psum x1 -> x0, blocking collectives: 39 us -> none  [on_device(): lax.psum((pack_symmetric(gramian(next_value)), jnp.concatenate([gramian(n...]
    reduce_scatter x1, waiting for transfers between devices: 24.5 us -> 0.01 us  [on_device(): lax.psum_scatter(grad_normed, 'head', scatter_dimension=2, tiled=True)]
  transfers between devices with their start and end apart: 14 -> 7, of which waited for: 12 -> 3; matrix products, arithmetic and copies ran while one was open for 12% -> 10% of each run, Pallas kernels for 0% -> 23%
where the time goes in v2:
time: 843 us; the launch traced here: 834 us
  Pallas kernels  530 us (63%)
  matrix products  100 us (12%)
  waiting for transfers between devices  67.9 us (8%)
  other arithmetic  49.3 us (6%)
  blocking collectives  36.9 us (4%)
  local copies, waits for them, and re-layouts  28.6 us (3%)
  between operations  16.1 us (2%)
    pallas_call x2, Pallas kernels, ring_scatter(): pl.pallas_call(functools.partial(ring_scatter_kernel, axis, count, arrays...  231 us
    pallas_call x2, Pallas kernels, ring_gather(): pl.pallas_call(functools.partial(ring_gather_kernel, axis, count, arrays,...  163 us
    pallas_call x2, Pallas kernels, orthogonal_rows(): pl.pallas_call(functools.partial(orthogonal_kernel, arrays, [len(strips)...  135 us
    psum x1, waiting for transfers between devices, on_device(): lax.psum(gram_strips(late_value) + [jnp.concatenate(gram_strips(next_bc)...  54.1 us
    dot_general x3, matrix products, back_project(): return jnp.einsum('stk,dk->std', upstream, weight, precision=PRECISE)  24.6 us
    dot_general x3, matrix products, project(): return jnp.einsum('std,dk->stk', activation, weight, precision=PRECISE)  20.2 us
    dot_general x3, matrix products, weight_grad(): return jnp.einsum('std,stk->dk', activation, upstream, precision=PRECISE)  17.9 us
  transfers between devices with their start and end apart: 7, of which 3 were waited for; matrix products, arithmetic and copies ran while one was open for 10% of the time, Pallas kernels for 23%

profile of v2, /device:TPU:0, one launch (start us, length us, event | category | flops | bytes accessed | tf_op | source)
XLA Modules:
  0.0 834.3 jit_solution(4093057151864338202)
XLA Ops:
  7.3 1.7 multiply_reduce_fusion.3
  11.3 58.5 %ring_gather_0.1 = f32[1536,896]{1,0:T(8,128)} custom-call(f32[192,896]{1,0:T(8,128)} %maximum_maximum_fusion.refs_0_), custom_call_target="tpu_custom_call" | custom-call | flops 28901376000 | bytes 9633792 | tf_op jit(solution)/shard_map/ring_gather_0/pallas_call | solution.py:193
  69.9 7.1 fusion.33
  78.0 3.4 collective-permute-start
  85.9 4.0 collective-permute-done
  89.9 4.5 fusion.62
  95.5 5.8 all_gather.12
  102.0 1.2 broadcast_multiply_fusion.6
  103.3 1.4 fusion.94
  105.5 104.5 %ring_gather_1.1 = (f32[1536,768]{1,0:T(8,128)}, f32[1536,768]{1,0:T(8,128)}, f32[768,128]{1,0:T(8,128)}) custom-call(f32[768,128]{1,0:T(8,128)} %bitcast.354, f32[768,128]{1,0:T(8,128)} %broadcast_in_dim.133.refs_1_, f32[192,768]{1,0:T(8,128)} %refs_2_.1, f32[192,768]{1,0:T(8,128)} %bitcast.353), custom_call_target="tpu_custom_call" | custom-call | flops 49545216000 | bytes 16515072 | tf_op jit(solution)/shard_map/ring_gather_1/pallas_call | solution.py:193
  210.1 2.4 broadcast_multiply_fusion.5
  212.6 2.2 fusion.51
  215.2 4.9 multiply_reduce_fusion.13
  220.0 6.2 psum.91
  226.3 8.2 multiply_reduce_fusion.9
  234.5 6.5 psum.92
  241.1 2.4 multiply_multiply_fusion.5
  243.6 1.1 fusion.63
  245.3 4.7 convolution_bitcast_fusion.refs_2_
  250.0 1.3 bitcast_multiply_fusion.2
  252.8 1.2 fusion.128.refs_0_
  254.0 6.1 fusion.15.refs_3_
  260.1 120.9 %ring_scatter_2.1 = (f32[192,768]{1,0:T(8,128)}, f32[192,768]{1,0:T(8,128)}, f32[768,128]{1,0:T(8,128)}) custom-call(f32[768,128]{1,0:T(8,128)} %fusion.128.refs_0_, f32[768,128]{1,0:T(8,128)} %broadcast_in_dim.133.refs_1_, f32[1536,768]{1,0:T(8,128)} %convolution_bitcast_fusion.refs_2_, f32[1536,768]{1,0:T(8,128)} %fusion.15.refs_3_), custom_call_target="tpu_custom_call" | custom-call | flops 56623104000 | bytes 18874368 | tf_op jit(solution)/shard_map/ring_scatter_2/pallas_call | solution.py:272
  381.1 1.4 multiply_add_fusion.1.refs_7_
  382.5 1.1 fusion.101
  383.6 1.2 fusion.81
  384.9 1.2 fusion.83
  386.2 1.5 fusion.109
  387.6 1.4 fusion.104
  389.1 4.5 fusion.8
  398.2 2.2 fusion.106
  401.7 1.5 copy.275
  403.2 1.2 dynamic-slice
  405.1 1.9 multiply_reduce_fusion.15
  407.0 1.4 reduce_sum.297
  408.4 1.3 reduce_sum.298
  409.7 2.5 multiply_reduce_fusion.8
  415.1 2.1 multiply_add_fusion.2
  417.2 7.5 convolution_bitcast_fusion.1
  427.6 4.4 fusion.45
  431.9 7.8 fusion.175
  440.6 4.1 fusion.167
  446.3 1.7 collective-permute-start.1
  448.1 2.1 pad_add_fusion
  450.4 9.8 %collective-permute-done.1 = f32[1,3,832]{1,2,0:T(8,128)S(1)} collective-permute-done((f32[1,3,832]{1,2,0:T(8,128)}, f32[1,3,832]{1,2,0:T(8,128)S(1)}, u32[]{:S(2)}, u32[]{:S(2)}) %collective-permute-start.1) | collective-permute-done | bytes 10016 | tf_op jit(solution)/shard_map/ppermute | solution.py:37
  460.1 1.7 slice_add_fusion
  461.9 7.2 fusion.13.refs_0_
  469.0 9.3 %multiply_reduce_fusion.2 = (f32[1536]{0:T(1024)S(1)}, f32[256]{0:T(256)}, f32[256,1536]{1,0:T(8,128)}) fusion(f32[1,256,1536]{2,1,0:T(8,128)S(1)} %copy-done, f32[256]{0:T(256)S(1)} %get-tuple-element.365, f32[1536]{0:T(1024)S(1)} %copy-done.52, f32[256,1536]{1,0:T(8,128)S(1)} %copy-done.18, f32[1536,896]{1,0:T(8,128)} %ring_gather_0.1, ...), kind=kOutput, calls=%fused_computation.29 | convolution fusion | flops 2117138688 | bytes 11105792 | tf_op jit(solution)/shard_map/stk,dk->std/dot_general | solution.py:301
  478.5 110.3 %ring_scatter_3.1 = f32[192,896]{1,0:T(8,128)} custom-call(f32[1536,896]{1,0:T(8,128)} %fusion.13.refs_0_), custom_call_target="tpu_custom_call" | custom-call | flops 33030144000 | bytes 11010048 | tf_op jit(solution)/shard_map/ring_scatter_3/pallas_call | solution.py:272
  593.0 5.8 all_gather.13
  598.9 7.1 psum.93
  607.5 2.0 multiply_add_fusion
  609.5 1.1 fusion.111
  610.6 1.2 fusion.85
  611.9 1.5 fusion.114
  613.4 84.5 %ortho_first.1 = (f32[192,768]{1,0:T(8,128)}, f32[192,768]{1,0:T(8,128)}) custom-call(f32[256,768]{1,0:T(8,128)} %get-tuple-element.311.refs_0_, f32[256,512]{1,0:T(8,128)} %get-tuple-element.312.refs_1_, f32[256,256]{1,0:T(8,128)} %get-tuple-element.313.refs_2_, f32[256,768]{1,0:T(8,128)} %get-tuple-element.314.refs_3_, ...), custom_call_target="tpu_custom_call" | custom-call | flops 77460406272 | tf_op jit(solution)/shard_map/ortho_first/pallas_call | solution.py:493
  697.9 2.0 multiply_subtract_fusion.2
  700.9 2.3 multiply_subtract_fusion.3
  703.2 54.1 %all-reduce.20.cloned.1.call-done = (f32[304,256]{1,0:T(8,128)}, f32[256,768]{1,0:T(8,128)}, f32[256,512]{1,0:T(8,128)}, f32[256,256]{1,0:T(8,128)}) async-done(((f32[304,256]{1,0:T(8,128)}, f32[256,768]{1,0:T(8,128)}, f32[256,512]{1,0:T(8,128)}, f32[256,256]{1,0:T(8,128)}), (f32[304,256]{1,0:T(8,128)}, f32[256,768]{1,0:T(8,128)}, f32[256,512]{1,0:T(8,128)}, ...) | async-done | bytes 1884176 | tf_op jit(solution)/shard_map/psum | solution.py:694
  758.7 1.7 slice.237.refs_3_
  760.4 5.4 all-gather
  766.8 50.9 %ortho_last.1 = (f32[192,768]{1,0:T(8,128)}, f32[192,256]{1,0:T(8,128)}, f32[192,128]{1,0:T(8,128)}) custom-call(f32[256,768]{1,0:T(8,128)} %get-tuple-element.308.refs_0_, f32[256,512]{1,0:T(8,128)} %get-tuple-element.309.refs_1_, f32[256,256]{1,0:T(8,128)} %get-tuple-element.310.refs_2_, f32[256,256]{1,0:T(8,128)} %slice.237.refs_3_, ...), custom_call_target="tpu_custom_call" | custom-call | flops 40674263040 | tf_op jit(solution)/shard_map/ortho_last/pallas_call | solution.py:493
  817.9 1.1 multiply_subtract_fusion.6
  819.7 2.0 multiply_subtract_fusion.1
  (372 shorter events, 43.0 us)
Async XLA Ops:
  7.2 432.5 %all-reduce.18.cloned.1.call-start = ((), (), s32[]{:S(2)}) async-start(), calls=%async_computation.4 | async-start | bytes 524288
  11.3 58.5 %copy-start = (f32[1,256,1536]{2,1,0:T(8,128)S(1)}, f32[1,256,1536]{2,1,0:T(8,128)}, u32[]{:S(2)}) copy-start(f32[1,256,1536]{2,1,0:T(8,128)} %param.22) | copy-start | bytes 4718596
  11.3 58.5 %copy-start.52 = (f32[1536]{0:T(1024)S(1)}, f32[1536]{0:T(1024)}, u32[]{:S(2)}) copy-start(f32[1536]{0:T(1024)} %param.29) | copy-start | bytes 18436
  69.8 11.6 %copy-start.106 = (f32[3,48]{1,0:T(4,128)S(1)}, f32[3,48]{1,0:T(4,128)}, u32[]{:S(2)}) copy-start(f32[3,48]{1,0:T(4,128)} %param.32) | copy-start | bytes 1732
  69.9 14.0 %copy-start.88 = (f32[5,256]{1,0:T(8,128)S(1)}, f32[5,256]{1,0:T(8,128)}, u32[]{:S(2)}) copy-start(f32[5,256]{1,0:T(8,128)} %param.31) | copy-start | bytes 15364
  76.9 17.5 %copy-start.2 = (f32[1,256,896]{1,2,0:T(8,128)}, f32[1,256,896]{1,2,0:T(8,128)S(1)}, u32[]{:S(2)}) copy-start(f32[1,256,896]{1,2,0:T(8,128)S(1)} %fusion.33) | copy-start | bytes 2752516
  78.0 11.9 %collective-permute-start = (f32[1,3,832]{1,2,0:T(8,128)}, f32[1,3,832]{1,2,0:T(8,128)S(1)}, u32[]{:S(2)}, u32[]{:S(2)}) collective-permute-start(f32[1,3,832]{1,2,0:T(8,128)} %slice.207), channel_id=1, source_target_pairs={{0,4},{4,8},{8,12},{12,16},{16,20},{20,24},{24,28},{1,5},{5,9},{9,... | collective-permute-start | bytes 29960 | tf_op jit(solution)/shard_map/ppermute | solution.py:37
  82.0 130.5 %copy-start.118 = (f32[12]{0:T(128)}, f32[12]{0:T(128)S(1)}, u32[]{:S(2)}) copy-start(f32[12]{0:T(128)S(1)} %get-tuple-element.362) | copy-start | bytes 148
  82.1 130.5 %copy-start.71 = (pred[256,256]{1,0:T(8,128)(4,1)}, pred[256,256]{1,0:T(8,128)(4,1)S(1)}, u32[]{:S(2)}) copy-start(pred[256,256]{1,0:T(8,128)(4,1)S(1)} %iota_compare_fusion.2) | copy-start | bytes 196612
  82.2 130.4 %copy-start.94 = (f32[12,256]{1,0:T(8,128)}, f32[12,256]{1,0:T(8,128)S(1)}, u32[]{:S(2)}) copy-start(f32[12,256]{1,0:T(8,128)S(1)} %fusion.166) | copy-start | bytes 36868
  82.4 306.7 %copy-start.62 = (f32[12,256]{1,0:T(8,128)}, f32[12,256]{1,0:T(8,128)S(1)}, u32[]{:S(2)}) copy-start(f32[12,256]{1,0:T(8,128)S(1)} %fusion.100) | copy-start | bytes 36868
  82.6 19.4 %copy-start.111 = (f32[12]{0:T(128)}, f32[12]{0:T(128)S(1)}, u32[]{:S(2)}) copy-start(f32[12]{0:T(128)S(1)} %get-tuple-element.367) | copy-start | bytes 148
  83.1 313.1 %copy-start.60 = (f32[256,12]{0,1:T(8,128)}, f32[256,12]{0,1:T(8,128)S(1)}, u32[]{:S(2)}) copy-start(f32[256,12]{0,1:T(8,128)S(1)} %get-tuple-element.360) | copy-start | bytes 36868
  85.9 8.6 %copy-start.77 = (f32[832]{0:T(1024)}, f32[832]{0:T(1024)S(1)}, u32[]{:S(2)}) copy-start(f32[832]{0:T(1024)S(1)} %get-tuple-element.299) | copy-start | bytes 9988
  85.9 8.6 %copy-start.79 = (f32[832]{0:T(1024)}, f32[832]{0:T(1024)S(1)}, u32[]{:S(2)}) copy-start(f32[832]{0:T(1024)S(1)} %get-tuple-element.300) | copy-start | bytes 9988
  85.9 8.6 %copy-start.81 = (f32[832]{0:T(1024)}, f32[832]{0:T(1024)S(1)}, u32[]{:S(2)}) copy-start(f32[832]{0:T(1024)S(1)} %get-tuple-element.301) | copy-start | bytes 9988
  85.9 8.6 %copy-start.83 = (f32[832]{0:T(1024)}, f32[832]{0:T(1024)S(1)}, u32[]{:S(2)}) copy-start(f32[832]{0:T(1024)S(1)} %get-tuple-element.302) | copy-start | bytes 9988
  89.9 5.5 copy-start.39
  101.7 294.1 %copy-start.28 = (f32[1,256,128]{2,1,0:T(8,128)}, f32[1,256,128]{2,1,0:T(8,128)S(1)}, u32[]{:S(2)}) copy-start(f32[1,256,128]{2,1,0:T(8,128)S(1)} %copy.294) | copy-start | bytes 393220
  102.0 110.6 %copy-start.54 = (f32[256,256]{1,0:T(8,128)}, f32[256,256]{1,0:T(8,128)S(1)}, u32[]{:S(2)}) copy-start(f32[256,256]{1,0:T(8,128)S(1)} %fusion.125) | copy-start | bytes 786436
  103.3 106.8 %copy-start.19 = (f32[12,64,128]{2,1,0:T(8,128)}, f32[12,64,128]{2,1,0:T(8,128)S(1)}, u32[]{:S(2)}) copy-start(f32[12,64,128]{2,1,0:T(8,128)S(1)} %get-tuple-element.369) | copy-start | bytes 1179652
  214.8 5.3 copy-start.33
  226.3 18.5 %copy-start.74 = (f32[1,256,1]{1,2,0:T(1,128)}, f32[1,256,1]{1,2,0:T(1,128)S(1)}, u32[]{:S(2)}) copy-start(f32[1,256,1]{1,2,0:T(1,128)S(1)} %get-tuple-element.336) | copy-start | bytes 3076
  243.6 10.4 %copy-start.10 = (f32[256,768]{0,1:T(8,128)}, f32[256,768]{0,1:T(8,128)S(1)}, u32[]{:S(2)}) copy-start(f32[256,768]{0,1:T(8,128)S(1)} %multiply_multiply_fusion.5) | copy-start | bytes 2359300
  245.3 6.0 copy-start.14
  382.5 5.2 copy-start.5
  389.1 4.8 copy-start.24
  398.1 211.3 %all-reduce.22.cloned.1.call-start = ((), (), s32[]{:S(2)}) async-start(), calls=%async_computation.6 | async-start | bytes 6291456 | tf_op jit(solution)/shard_map/psum | solution.py:689
  400.4 300.5 %reduce-scatter.3.cloned.1.call-start = ((), (), s32[]{:S(2)}) async-start(), calls=%async_computation.2 | async-start | bytes 1966080 | tf_op jit(solution)/shard_map/reduce_scatter | solution.py:591
  401.7 11.4 %copy-start.21 = (f32[12,64,128]{2,1,0:T(8,128)S(1)}, f32[12,64,128]{2,1,0:T(8,128)}, u32[]{:S(2)}) copy-start(f32[12,64,128]{2,1,0:T(8,128)} %copy-done.19) | copy-start | bytes 1179652
  424.9 275.9 %reduce-scatter.5.cloned.1.call-start = ((), (), s32[]{:S(2)}) async-start(), calls=%async_computation.3 | async-start | bytes 1966080 | tf_op jit(solution)/shard_map/reduce_scatter | solution.py:654
  431.9 8.6 %copy-start.40 = (f32[1,3,832]{1,2,0:T(8,128)S(1)}, f32[1,3,832]{1,2,0:T(8,128)}, u32[]{:S(2)}) copy-start(f32[1,3,832]{1,2,0:T(8,128)} %copy-done.39) | copy-start | bytes 29956
  446.3 13.8 %collective-permute-start.1 = (f32[1,3,832]{1,2,0:T(8,128)}, f32[1,3,832]{1,2,0:T(8,128)S(1)}, u32[]{:S(2)}, u32[]{:S(2)}) collective-permute-start(f32[1,3,832]{1,2,0:T(8,128)} %pad_add_fusion.1), channel_id=1, source_target_pairs={{4,0},{8,4},{12,8},{16,12},{20,16},{24,20},{28,24},{5,1},{9,5},{13... | collective-permute-start | bytes 29960 | tf_op jit(solution)/shard_map/ppermute | solution.py:37
  450.2 11.6 %copy-start.67 = (f32[896]{0:T(1024)S(1)}, f32[896]{0:T(1024)}, u32[]{:S(2)}) copy-start(f32[896]{0:T(1024)} %copy-done.66) | copy-start | bytes 10756
  461.9 7.2 copy-start.18
  478.4 111.3 %copy-start.50 = (f32[192,12]{1,0:T(8,128)S(1)}, f32[192,12]{1,0:T(8,128)}, u32[]{:S(2)}) copy-start(f32[192,12]{1,0:T(8,128)} %copy.275) | copy-start | bytes 27652
  478.4 113.7 %copy-start.90 = (f32[768]{0:T(1024)S(1)}, f32[768]{0:T(1024)}, u32[]{:S(2)}) copy-start(f32[768]{0:T(1024)} %get-tuple-element.289) | copy-start | bytes 9220
  478.4 113.7 %copy-start.113 = (f32[12]{0:T(128)S(1)}, f32[12]{0:T(128)}, u32[]{:S(2)}) copy-start(f32[12]{0:T(128)} %reduce_sum.309) | copy-start | bytes 148
  478.4 113.7 %copy-start.116 = (f32[12]{0:T(128)S(1)}, f32[12]{0:T(128)}, u32[]{:S(2)}) copy-start(f32[12]{0:T(128)} %get-tuple-element.330) | copy-start | bytes 148
  478.4 113.6 %copy-start.117 = (f32[12]{0:T(128)S(1)}, f32[12]{0:T(128)}, u32[]{:S(2)}) copy-start(f32[12]{0:T(128)} %get-tuple-element.343) | copy-start | bytes 148
  478.5 278.8 %all-reduce.20.cloned.1.call-start = ((), (), s32[]{:S(2)}) async-start(), calls=%async_computation.5 | async-start | bytes 3768320 | tf_op jit(solution)/shard_map/psum | solution.py:694
  588.8 10.1 %copy-start.110 = (f32[256]{0:T(256)S(1)}, f32[256]{0:T(256)}, u32[]{:S(2)}) copy-start(f32[256]{0:T(256)} %get-tuple-element.285) | copy-start | bytes 3076
  588.8 17.5 %copy-start.57 = (f32[192,256]{1,0:T(8,128)S(1)}, f32[192,256]{1,0:T(8,128)}, u32[]{:S(2)}) copy-start(f32[192,256]{1,0:T(8,128)} %param.36) | copy-start | bytes 589828
  592.2 15.3 %copy-start.41 = (f32[192,896]{1,0:T(8,128)S(1)}, f32[192,896]{1,0:T(8,128)}, u32[]{:S(2)}) copy-start(f32[192,896]{1,0:T(8,128)} %ring_scatter_3.1) | copy-start | bytes 2064388
  598.9 10.6 %copy-start.44 = (f32[192,256]{1,0:T(8,128)}, f32[192,256]{1,0:T(8,128)S(1)}, u32[]{:S(2)}) copy-start(f32[192,256]{1,0:T(8,128)S(1)} %copy.278) | copy-start | bytes 589828
  613.3 84.5 %copy-start.45 = (f32[192,768]{1,0:T(8,128)S(1)}, f32[192,768]{1,0:T(8,128)}, u32[]{:S(2)}) copy-start(f32[192,768]{1,0:T(8,128)} %refs_2_.1) | copy-start | bytes 1769476
  765.9 56.9 %copy-start.86 = (f32[1536]{0:T(1024)}, f32[1536]{0:T(1024)S(1)}, u32[]{:S(2)}) copy-start(f32[1536]{0:T(1024)S(1)} %slice_reduce_fusion) | copy-start | bytes 18436
  766.2 58.5 %copy-start.51 = (f32[4,5,768]{2,1,0:T(8,128)}, f32[4,5,768]{2,1,0:T(8,128)S(1)}, u32[]{:S(2)}) copy-start(f32[4,5,768]{2,1,0:T(8,128)S(1)} %slice.223) | copy-start | bytes 184324
  766.8 51.0 %copy-start.43 = (f32[192,12]{1,0:T(8,128)S(1)}, f32[192,12]{1,0:T(8,128)}, u32[]{:S(2)}) copy-start(f32[192,12]{1,0:T(8,128)} %copy-done.42) | copy-start | bytes 27652
  766.8 52.9 %copy-start.37 = (f32[192,768]{1,0:T(8,128)S(1)}, f32[192,768]{1,0:T(8,128)}, u32[]{:S(2)}) copy-start(f32[192,768]{1,0:T(8,128)} %param.25) | copy-start | bytes 1769476
  817.8 5.0 copy-start.53
  817.8 5.0 copy-start.104
  817.8 5.6 copy-start.87
  817.8 5.6 copy-start.98
  817.8 6.2 copy-start.89
  817.8 6.2 copy-start.105
  817.8 6.8 copy-start.59
  817.8 6.8 copy-start.65
  819.0 6.4 copy-start.107
  819.0 6.4 copy-start.115
  819.7 6.3 copy-start.35
  821.7 5.1 copy-start.23
  822.0 5.6 copy-start.76
  822.1 5.5 copy-start.85
  (69 other events, 163.2 us)
Sparse Core Ops, SparseCore 0:
  398.3 29.2 all-reduce.17
  432.4 161.8 all-reduce.21
  596.8 27.9 reduce-scatter.2
  627.2 28.0 reduce-scatter.4
  659.7 97.5 all-reduce.19

commit v3 on v2

--- a/solution.py
+++ b/solution.py
@@ -122,26 +122,39 @@
     return me, place, right, left
 
 
+def halves(value):
+    high = value.astype(jnp.bfloat16)
+    return high, (value - high.astype(jnp.float32)).astype(jnp.bfloat16)
+
+
+def three_pass(left, right, contract=(1, 0)):
+    def one(a, b):
+        dims = (((contract[0],), (contract[1],)), ((), ()))
+        return lax.dot_general(a, b, dims, preferred_element_type=jnp.float32)
+
+    return one(left[0], right[0]) + (one(left[0], right[1]) + one(left[1], right[0]))
+
+
 def ring_gather_kernel(axis, count, arrays, backward, *refs):
     relayed = backward is not None
     turn, finish = (lambda at: None), (lambda: None)
     if relayed:
         states, refs = refs[:2], refs[2:]
-        near, refs = refs[2 * arrays], refs[: 2 * arrays] + refs[2 * arrays + 1 :]
+        near, refs = refs[4 * arrays], refs[: 4 * arrays] + refs[4 * arrays + 1 :]
         turn, finish = relay_step(axis, count, backward, (*states, near, *refs[-4:]))
         refs = refs[:-4]
-    shards, outs = refs[:arrays], refs[arrays : 2 * arrays]
-    send_sem, recv_sem, own_sem = refs[2 * arrays :]
+    shards, lefts, outs, products, holds = (
+        refs[at * arrays : (at + 1) * arrays] for at in range(5)
+    )
+    send_sem, recv_sem, store_sem, own_sem = refs[5 * arrays :]
     me, place, right, left = ring_neighbours(axis, count, relayed)
-    own = []
-    for j in range(arrays):
-        rows = shards[j].shape[0]
-        start = pl.multiple_of(me * rows, 8)
-        own.append(
-            pltpu.make_async_copy(shards[j], outs[j].at[pl.ds(start, rows)], own_sem.at[j])
-        )
+    stores = []
+
+    def product(j, block, region):
+        return three_pass(halves(lefts[j][region, :]), halves(block[...]), (0, 0))
+
     flights = {}
-    for step in range(count - 1):
+    for step in range(count):
         for j in range(arrays):
             rows = shards[j].shape[0]
             pieces = piece_count(rows // 2, arrays)
@@ -153,29 +166,40 @@
                     region = pl.ds(pl.multiple_of(origin * rows + within, 8), length)
                     if step:
                         flights[step - 1, j, piece, way].wait_recv()
-                        source = outs[j].at[region]
+                        source = holds[j].at[region]
                     else:
                         source = shards[j].at[pl.ds(within, length)]
-                    flight = pltpu.make_async_remote_copy(
-                        src_ref=source,
-                        dst_ref=outs[j].at[region],
-                        send_sem=send_sem.at[way, j + piece, step],
-                        recv_sem=recv_sem.at[way, j + piece, step],
-                        device_id={axis: target},
-                        device_id_type=pl.DeviceIdType.MESH,
-                    )
-                    flights[step, j, piece, way] = flight
-                    flight.start()
+                    if step < count - 1:
+                        flight = pltpu.make_async_remote_copy(
+                            src_ref=source,
+                            dst_ref=holds[j].at[region],
+                            send_sem=send_sem.at[way, j + piece, step],
+                            recv_sem=recv_sem.at[way, j + piece, step],
+                            device_id={axis: target},
+                            device_id_type=pl.DeviceIdType.MESH,
+                        )
+                        flights[step, j, piece, way] = flight
+                        flight.start()
+                    if step:
+                        store = pltpu.make_async_copy(
+                            source, outs[j].at[region], store_sem.at[way, j + piece, step - 1]
+                        )
+                        stores.append(store)
+                        store.start()
+                        products[j][...] += product(j, source, region)
         if step == 0:
-            for copy in own:
-                copy.start()
-        turn(step)
-    for (step, *_), flight in flights.items():
-        if step == count - 2:
-            flight.wait_recv()
+            for j in range(arrays):
+                rows = shards[j].shape[0]
+                region = pl.ds(pl.multiple_of(me * rows, 8), rows)
+                store = pltpu.make_async_copy(shards[j], outs[j].at[region], own_sem.at[j])
+                stores.append(store)
+                store.start()
+                products[j][...] = product(j, shards[j], region)
+        if step < count - 1:
+            turn(step)
     finish()
-    for copy in own:
-        copy.wait()
+    for store in stores:
+        store.wait()
     for flight in flights.values():
         flight.wait_send()
 
@@ -184,23 +208,27 @@
     return pl.CostEstimate(flops=6000 * sent, bytes_accessed=2 * sent, transcendentals=0)
 
 
-def ring_gather(shards, axis, collective_id, relay=None):
+def ring_gather(shards, lefts, axis, collective_id, relay=None):
     count = lax.axis_size(axis)
     arrays = len(shards)
     states, near, relay_scratch = relay_parts(relay)
     backward = None if relay is None else relay[2]
     sent = sum(shard.size for shard in shards) * 4 * (count - 1)
+    whole = [(count * shard.shape[0], shard.shape[1]) for shard in shards]
     return pl.pallas_call(
         functools.partial(ring_gather_kernel, axis, count, arrays, backward),
-        out_shape=[
-            jax.ShapeDtypeStruct((count * shard.shape[0], shard.shape[1]), shard.dtype)
-            for shard in shards
+        out_shape=[jax.ShapeDtypeStruct(shape, jnp.float32) for shape in whole]
+        + [
+            jax.ShapeDtypeStruct((left.shape[1], shard.shape[1]), jnp.float32)
+            for left, shard in zip(lefts, shards)
         ]
         + near,
-        in_specs=[pl.BlockSpec(memory_space=pltpu.VMEM)] * (arrays + len(states)),
+        in_specs=[pl.BlockSpec(memory_space=pltpu.VMEM)] * (2 * arrays + len(states)),
         out_specs=[pl.BlockSpec(memory_space=pl.ANY)] * arrays
-        + [pl.BlockSpec(memory_space=pltpu.VMEM)] * len(near),
-        scratch_shapes=[
+        + [pl.BlockSpec(memory_space=pltpu.VMEM)] * (arrays + len(near)),
+        scratch_shapes=[pltpu.VMEM(shape, jnp.float32) for shape in whole]
+        + [
+            pltpu.SemaphoreType.DMA((2, max(arrays, 2), count - 1)),
             pltpu.SemaphoreType.DMA((2, max(arrays, 2), count - 1)),
             pltpu.SemaphoreType.DMA((2, max(arrays, 2), count - 1)),
             pltpu.SemaphoreType.DMA((arrays,)),
@@ -209,7 +237,7 @@
         compiler_params=pltpu.CompilerParams(collective_id=collective_id, has_side_effects=True),
         cost_estimate=busy_cost(sent),
         name=f"ring_gather_{collective_id}",
-    )(*states, *shards)
+    )(*states, *shards, *lefts)
 
 
 def ring_scatter_kernel(axis, count, arrays, backward, *refs):
@@ -217,11 +245,15 @@
     turn, finish = (lambda at: None), (lambda: None)
     if relayed:
         states, refs = refs[:2], refs[2:]
-        near, refs = refs[2 * arrays], refs[: 2 * arrays] + refs[2 * arrays + 1 :]
+        near, refs = refs[3 * arrays], refs[: 3 * arrays] + refs[3 * arrays + 1 :]
         turn, finish = relay_step(axis, count, backward, (*states, near, *refs[-4:]))
         refs = refs[:-4]
-    parts, outs, slots = refs[:arrays], refs[arrays : 2 * arrays], refs[2 * arrays : 3 * arrays]
-    send_sem, recv_sem = refs[3 * arrays :]
+    lefts, rights, outs, slots, firsts, highs, lows = (
+        refs[at * arrays : (at + 1) * arrays] for at in range(7)
+    )
+    send_sem, recv_sem = refs[7 * arrays :]
+    for j in range(arrays):
+        highs[j][...], lows[j][...] = halves(rights[j][...])
     me, place, right, left = ring_neighbours(axis, count, relayed)
     flights = {}
     for step in range(count):
@@ -235,16 +267,20 @@
                     goal = ring_index(place + sign * (1 + step), count)
                     within = (way * pieces + piece) * length
                     region = pl.ds(pl.multiple_of(goal * rows + within, 8), length)
+                    block = three_pass(
+                        halves(lefts[j][region, :]), (highs[j][...], lows[j][...])
+                    )
                     if step:
                         flights[step - 1, j, piece, way].wait_recv()
-                        total = slots[j][way, step - 1, part, :] + parts[j][region, :]
+                        total = slots[j][way, step - 1, part, :] + block
                         if step == count - 1:
                             outs[j][pl.ds(within, length), :] = total
                             continue
                         slots[j][way, step - 1, part, :] = total
                         source = slots[j].at[way, step - 1, part]
                     else:
-                        source = parts[j].at[region]
+                        firsts[j][way, part, :] = block
+                        source = firsts[j].at[way, part]
                     flight = pltpu.make_async_remote_copy(
                         src_ref=source,
                         dst_ref=slots[j].at[way, step, part],
@@ -262,21 +298,23 @@
         flight.wait_send()
 
 
-def ring_scatter(parts, axis, collective_id, relay=None):
+def ring_scatter(factors, axis, collective_id, relay=None):
     count = lax.axis_size(axis)
-    arrays = len(parts)
+    arrays = len(factors)
     states, near, relay_scratch = relay_parts(relay)
     backward = None if relay is None else relay[2]
-    shapes = [(part.shape[0] // count, part.shape[1]) for part in parts]
-    sent = sum(part.size for part in parts) * 4
+    shapes = [(left.shape[0] // count, right.shape[1]) for left, right in factors]
+    sent = sum(rows * columns for rows, columns in shapes) * 4 * count
     return pl.pallas_call(
         functools.partial(ring_scatter_kernel, axis, count, arrays, backward),
         out_shape=[jax.ShapeDtypeStruct(shape, jnp.float32) for shape in shapes] + near,
-        in_specs=[pl.BlockSpec(memory_space=pltpu.VMEM)] * (arrays + len(states)),
+        in_specs=[pl.BlockSpec(memory_space=pltpu.VMEM)] * (2 * arrays + len(states)),
         out_specs=[pl.BlockSpec(memory_space=pltpu.VMEM)] * (arrays + len(near)),
         scratch_shapes=[
             pltpu.VMEM((2, count - 1, rows // 2, columns), jnp.float32) for rows, columns in shapes
         ]
+        + [pltpu.VMEM((2, rows // 2, columns), jnp.float32) for rows, columns in shapes]
+        + [pltpu.VMEM(right.shape, jnp.bfloat16) for _, right in factors] * 2
         + [
             pltpu.SemaphoreType.DMA((2, max(arrays, 2), count - 1)),
             pltpu.SemaphoreType.DMA((2, max(arrays, 2), count - 1)),
@@ -285,7 +323,7 @@
         compiler_params=pltpu.CompilerParams(collective_id=collective_id, has_side_effects=True),
         cost_estimate=busy_cost(sent),
         name=f"ring_scatter_{collective_id}",
-    )(*states, *parts)
+    )(*states, *[left for left, _ in factors], *[right for _, right in factors])
 
 
 def silu_grad(pre_value):
@@ -381,18 +419,6 @@
     output = base_out + entry_term(entry_state, log_decay, c_state)
     leaving = decay_all[..., None, None] * entry_state + summary
     return (output, leaving)
-
-
-def halves(value):
-    high = value.astype(jnp.bfloat16)
-    return high, (value - high.astype(jnp.float32)).astype(jnp.bfloat16)
-
-
-def three_pass(left, right):
-    def one(a, b):
-        return jnp.dot(a, b, preferred_element_type=jnp.float32)
-
-    return one(left[0], right[0]) + (one(left[0], right[1]) + one(left[1], right[0]))
 
 
 def gram_strips(rows):
@@ -545,14 +571,16 @@
         ],
         axis=1,
     )
-    (mixed_full,) = ring_gather((side_mine,), "seq", 0)
     conv_mine = lax.dynamic_slice_in_dim(conv_value, head_index * inner_width, inner_width, 1)
     gain_mine = lax.dynamic_slice_in_dim(out_gain, head_index * inner_width, inner_width, 0)
     head_mine = lax.dynamic_slice_in_dim(head_params, head_index * local_heads, local_heads, 1)
     bc_taps = lax.dynamic_slice_in_dim(conv_bc, head_index * bc_width, bc_width, 1)
     inv_rms = lax.rsqrt(jnp.mean(block_input * block_input, axis=-1, keepdims=True) + EPSILON)
     normed = block_input * inv_rms * in_gain
-    all_pre = project(normed, mixed_full)
+    normed_turned = normed[0].T
+    cotangent_turned = cotangent[0].T
+    mixed_full, all_pre = ring_gather((side_mine,), (normed_turned,), "seq", 0)
+    all_pre = all_pre[None]
     mixed_width = inner_width + bc_width
     mixed_pre = all_pre[..., :mixed_width]
     step_pre = all_pre[..., mixed_width : mixed_width + local_heads]
@@ -578,37 +606,42 @@
     state_shape = summary.shape
     state_rows = (-1, state_shape[-1])
     decay_rows = jnp.broadcast_to(decay_all[..., None, None], state_shape).reshape(state_rows)
-    gate_full, out_full, entry_rows = ring_gather(
-        (gate_proj, out_proj.T), "seq", 1, (summary.reshape(state_rows), decay_rows, False)
-    )
+    gate_full, out_full, gate_pre, grad_normout, entry_rows = ring_gather(
+        (gate_proj, out_proj.T),
+        (normed_turned, cotangent_turned),
+        "seq",
+        1,
+        (summary.reshape(state_rows), decay_rows, False),
+    )
+    gate_pre, grad_normout = gate_pre[None], grad_normout[None]
     entry_state = entry_rows.reshape(state_shape)
-    gate_pre = project(normed, gate_full)
     mixer_out = base_out + entry_term(entry_state, log_decay, c_state)
     gate_act = jax.nn.silu(gate_pre)
     gated = mixer_out * gate_act
     square_part = jnp.sum(gated * gated, axis=-1, keepdims=True)
     out_part = back_project(gated * gain_mine, out_full)
     out_sum = lax.psum_scatter(out_part, "head", scatter_dimension=2, tiled=True)
-    square_sum = lax.psum(square_part, "head")
+    scaled = grad_normout * gain_mine
+    dot_part = jnp.sum(scaled * gated, axis=-1, keepdims=True)
+    square_sum, dot_total = lax.psum((square_part, dot_part), "head")
     gate_rms = lax.rsqrt(square_sum / DI + EPSILON)
     input_mine = lax.dynamic_slice_in_dim(block_input, head_index * model_part, model_part, 2)
     cotangent_mine = lax.dynamic_slice_in_dim(cotangent, head_index * model_part, model_part, 2)
-    block_output = input_mine + gate_rms * out_sum
     normed_out = gated * gate_rms * gain_mine
-    grad_outfull = weight_grad(cotangent, normed_out)
-    grad_normout = project(cotangent, out_full)
     grad_outgain_mine = jnp.sum(grad_normout * gated * gate_rms, axis=(0, 1))
-    scaled = grad_normout * gain_mine
-    dot_total = lax.psum(jnp.sum(scaled * gated, axis=-1, keepdims=True), "head")
     grad_gated = gate_rms * scaled - gate_rms**3 * gated * dot_total / DI
     grad_mixer = grad_gated * gate_act
     grad_gate_pre = grad_gated * mixer_out * silu_grad(gate_pre)
-    grad_gatefull = weight_grad(normed, grad_gate_pre)
     _, entry_back = jax.vjp(lambda entering: entry_term(entering, log_decay, c_state), entry_state)
     direct = entry_back(grad_mixer)[0]
     grad_out_rows, grad_gate, leave_rows = ring_scatter(
-        (grad_outfull, grad_gatefull), "seq", 2, (direct.reshape(state_rows), decay_rows, True)
-    )
+        ((cotangent_turned, normed_out[0]), (normed_turned, grad_gate_pre[0])),
+        "seq",
+        2,
+        (direct.reshape(state_rows), decay_rows, True),
+    )
+    leave_rows, out_sum = lax.optimization_barrier((leave_rows, out_sum))
+    block_output = input_mine + gate_rms * out_sum
     leave_grad = leave_rows.reshape(state_shape)
     _, mixer_back = jax.vjp(
         full_mixer, values, step_size, log_decay, b_state, c_state, skip_gain, entry_state
@@ -648,19 +681,10 @@
         ],
         axis=-1,
     )
-    grad_mixedfull = weight_grad(normed, grad_all_pre)
     grad_normed = back_project(grad_gate_pre, gate_full) + back_project(grad_all_pre, mixed_full)
     stat_part = jnp.sum(grad_normed * in_gain * block_input, axis=-1, keepdims=True)
-    normed_grad_mine = lax.psum_scatter(grad_normed, "head", scatter_dimension=2, tiled=True)
-    stat_total = lax.psum(stat_part, "head")
-    gain_part = lax.dynamic_slice_in_dim(in_gain, head_index * model_part, model_part, 0)
-    input_grad = (
-        cotangent_mine
-        + inv_rms * gain_part * normed_grad_mine
-        - inv_rms**3 * input_mine * stat_total / D
-    )
     grad_ingain_part = jnp.sum(grad_normed * block_input * inv_rms, axis=(0, 1))
-    (grad_mixed_rows,) = ring_scatter((grad_mixedfull,), "seq", 3)
+    (grad_mixed_rows,) = ring_scatter(((normed_turned, grad_all_pre[0]),), "seq", 3)
     grad_value = grad_mixed_rows[:, :inner_width]
     grad_bc = lax.all_gather(
         grad_mixed_rows[:, inner_width:mixed_width], "head", axis=1, tiled=True
@@ -722,7 +746,18 @@
     update_out, update_gate = orthogonal_rows(
         ((out_gram, next_out_rows), (gate_gram, next_gate)), "ortho_first"
     )
+    grad_normed, stat_part, update_out = lax.optimization_barrier(
+        (grad_normed, stat_part, update_out)
+    )
     update_out = update_out.T
+    normed_grad_mine = lax.psum_scatter(grad_normed, "head", scatter_dimension=2, tiled=True)
+    stat_total = lax.psum(stat_part, "head")
+    gain_part = lax.dynamic_slice_in_dim(in_gain, head_index * model_part, model_part, 0)
+    input_grad = (
+        cotangent_mine
+        + inv_rms * gain_part * normed_grad_mine
+        - inv_rms**3 * input_mine * stat_total / D
+    )
     update_value, update_bc, update_step = orthogonal_rows(
         (
             (value_gram, next_value),

time: 843 us -> 830 us (0.985)
  matrix products: 100 us -> 60.5 us
  local copies, waits for them, and re-layouts: 28.6 us -> 49.2 us
  waiting for transfers between devices: 67.9 us -> 79.6 us
  Pallas kernels: 530 us -> 519 us
    psum x1, waiting for transfers between devices: 0.02 us -> 60.5 us  [on_device(): early = lax.psum(gram_strips(next_out_rows) + gram_strips(next_gate), 'seq')]
    psum x1, waiting for transfers between devices: 54.1 us -> 0.02 us  [on_device(): lax.psum(gram_strips(late_value) + [jnp.concatenate(gram_strips(next_bc)...]
    dot_general x6 -> x0, matrix products: 38.1 us -> none  [the longest x3 20.2 us: project(): return jnp.einsum('std,dk->stk', activation, weight, precision=PRECISE)]
    unnamed x6, waiting for transfers between devices: 0.08 us -> 15.9 us
    pallas_call x2, Pallas kernels: 231 us -> 220 us  [ring_scatter(): pl.pallas_call(functools.partial(ring_scatter_kernel, axis, count, arrays...]
    ppermute x2, waiting for transfers between devices: 13.7 us -> 3.22 us  [from_behind(): lax.ppermute(value, axis, [(source, source + steps) for source in range(i...]
  transfers between devices with their start and end apart: 7 -> 7, of which waited for: 3 -> 3; matrix products, arithmetic and copies ran while one was open for 10% -> 10% of each run, Pallas kernels for 23% -> 43%
where the time goes in v3:
time: 830 us; the launch traced here: 820 us
  Pallas kernels  519 us (63%)
  waiting for transfers between devices  79.6 us (10%)
  matrix products  60.5 us (7%)
  other arithmetic  51.2 us (6%)
  local copies, waits for them, and re-layouts  49.2 us (6%)
  blocking collectives  38.2 us (5%)
  between operations  16.2 us (2%)
    pallas_call x2, Pallas kernels, ring_scatter(): pl.pallas_call(functools.partial(ring_scatter_kernel, axis, count, arrays...  220 us
    pallas_call x2, Pallas kernels, ring_gather(): pl.pallas_call(functools.partial(ring_gather_kernel, axis, count, arrays,...  164 us
    pallas_call x2, Pallas kernels, orthogonal_rows(): pl.pallas_call(functools.partial(orthogonal_kernel, arrays, [len(strips)...  136 us
    psum x1, waiting for transfers between devices, on_device(): early = lax.psum(gram_strips(next_out_rows) + gram_strips(next_gate), 'seq')  60.5 us
  transfers between devices with their start and end apart: 7, of which 3 were waited for; matrix products, arithmetic and copies ran while one was open for 10% of the time, Pallas kernels for 43%

profile of v3, /device:TPU:0, one launch (start us, length us, event | category | flops | bytes accessed | tf_op | source)
XLA Modules:
  0.0 820.1 jit_solution(17733464481235542935)
XLA Ops:
  7.3 2.0 copy.281
  10.4 1.5 multiply_bitcast_fusion.refs_1_.refs_4_.refs_3_.refs_0_
  12.9 61.2 %ring_gather_0.1 = (f32[1536,896]{1,0:T(8,128)}, f32[256,896]{1,0:T(8,128)}) custom-call(f32[192,896]{1,0:T(8,128)} %maximum_maximum_fusion.refs_0_, f32[1536,256]{1,0:T(8,128)} %multiply_bitcast_fusion.refs_1_.refs_4_.refs_3_.refs_0_), custom_call_target="tpu_custom_call" | custom-call | flops 28901376000 | bytes 9633792 | tf_op jit(solution)/shard_map/ring_gather_0/pallas_call | solution.py:218
  74.1 1.4 slice.207
  75.5 4.1 collective-permute-start
  80.1 1.2 fusion.69
  84.4 1.3 constant_dynamic-slice_fusion.3
  88.9 1.6 copy.293
  91.4 1.4 dynamic_slice.29
  92.8 1.2 copy.300
  95.3 1.4 dynamic_slice.31
  98.8 2.4 fusion.44
  102.3 6.1 all_gather.12
  109.4 1.2 broadcast_multiply_fusion.6
  111.9 4.0 fusion.34
  115.9 2.3 copy.295
  119.1 103.0 %ring_gather_1.1 = (f32[1536,768]{1,0:T(8,128)}, f32[1536,768]{1,0:T(8,128)}, f32[256,768]{1,0:T(8,128)}, f32[256,768]{1,0:T(8,128)}, f32[768,128]{1,0:T(8,128)}) custom-call(f32[768,128]{1,0:T(8,128)} %bitcast.341, f32[768,128]{1,0:T(8,128)} %broadcast_in_dim.139.refs_1_, f32[192,768]{1,0:T(8,128)} %refs_2_.1, f32[192,768]{1,0:T(8,128)} %bitcast.340, ...), custom_call_target="tpu_custom_call" | custom-call | flops 49545216000 | bytes 16515072 | tf_op jit(solution)/shard_map/ring_gather_1/pallas_call | solution.py:218
  222.1 2.4 broadcast_multiply_fusion.5
  225.7 3.1 multiply_reduce_fusion.13
  228.7 6.4 psum.91
  235.7 1.9 multiply_reduce_fusion.9
  237.6 6.6 psum.92
  244.2 2.7 fusion.45
  246.9 3.0 multiply_multiply_fusion
  251.1 2.2 mul.725
  253.3 2.3 copy.301
  255.6 2.5 multiply_reduce_fusion.10
  258.1 1.2 fusion.110.refs_0_
  259.3 5.5 convolution_bitcast_fusion
  265.1 1.5 copy.308
  267.4 5.6 fusion.7
  275.3 121.3 %ring_scatter_2.1 = (f32[192,768]{1,0:T(8,128)}, f32[192,768]{1,0:T(8,128)}, f32[768,128]{1,0:T(8,128)}) custom-call(f32[768,128]{1,0:T(8,128)} %fusion.110.refs_0_, f32[768,128]{1,0:T(8,128)} %broadcast_in_dim.139.refs_1_, f32[1536,256]{1,0:T(8,128)} %bitcast.337, f32[1536,256]{1,0:T(8,128)} %multiply_bitcast_fusion.refs_1_.refs_4_.refs_3_.refs_0_, ...), custom_call_target="tpu_custom_call" | custom-call | flops 56623104000 | bytes 18874368 | tf_op jit(solution)/shard_map/ring_scatter_2/pallas_call | solution.py:308
  397.3 2.0 convolution_bitcast_fusion.2
  399.3 1.6 convolution_bitcast_fusion.3
  401.0 1.9 fusion.46
  407.6 1.4 fusion.78
  409.1 1.4 fusion.73
  411.4 3.3 fusion.143
  414.8 1.5 fusion.37
  420.3 1.5 multiply_reduce_fusion.8
  421.8 1.3 multiply_reduce_fusion.14
  424.0 1.4 convolution_add_fusion.2
  425.6 3.8 fusion.28
  429.4 1.5 copy.305
  431.8 15.8 %all-reduce.18.cloned.1.call-done = f32[1,256,256]{1,0,2:T(1,128)} async-done(((f32[1,256,256]{1,0,2:T(1,128)}), f32[1,256,256]{1,0,2:T(1,128)}) %all-reduce.18.cloned.1.call-update) | async-done | bytes 262160
  448.5 1.6 fusion.136
  450.5 1.3 collective-permute-start.1
  452.9 3.2 collective-permute-done.1
  457.3 98.4 %ring_scatter_3.1 = f32[192,896]{1,0:T(8,128)} custom-call(f32[1536,256]{1,0:T(8,128)} %multiply_bitcast_fusion.refs_1_.refs_4_.refs_3_.refs_0_, f32[256,896]{1,0:T(8,128)} %maximum_bitcast_fusion.refs_1_), custom_call_target="tpu_custom_call" | custom-call | flops 33030144000 | bytes 11010048 | tf_op jit(solution)/shard_map/ring_scatter_3/pallas_call | solution.py:308
  555.7 2.3 multiply_add_fusion
  558.0 60.5 %all-reduce.22.cloned.1.call-done = (f32[256,768]{1,0:T(8,128)}, f32[256,512]{1,0:T(8,128)}, f32[256,256]{1,0:T(8,128)}, f32[256,768]{1,0:T(8,128)}, f32[256,512]{1,0:T(8,128)}, /*index=5*/f32[256,256]{1,0:T(8,128)}) async-done(((f32[256,768]{1,0:T(8,128)}, f32[256,512]{1,0:T(8,128)}, f32[256,256]{1,0:T(8,128)}, f32[256,768]{1,0:T(8,128)}, f32[256,512]{1,0:T(8,128)}, /*index=5*/f32[256,256]{1,0:T(8,128)}), ...) | async-done | bytes 3145744 | tf_op jit(solution)/shard_map/psum | solution.py:713
  618.5 1.4 fusion.83
  622.4 5.8 all_gather.13
  629.7 7.7 multiply_reduce_fusion.2
  640.4 84.7 %ortho_first.1 = (f32[192,768]{1,0:T(8,128)}, f32[192,768]{1,0:T(8,128)}) custom-call(f32[256,768]{1,0:T(8,128)} %get-tuple-element.295.refs_0_, f32[256,512]{1,0:T(8,128)} %get-tuple-element.296.refs_1_, f32[256,256]{1,0:T(8,128)} %get-tuple-element.297.refs_2_, f32[256,768]{1,0:T(8,128)} %get-tuple-element.298.refs_3_, ...), custom_call_target="tpu_custom_call" | custom-call | flops 77460406272 | tf_op jit(solution)/shard_map/ortho_first/pallas_call | solution.py:519
  725.2 2.0 multiply_subtract_fusion.2
  729.2 8.0 psum.99
  737.2 1.9 bitcast_subtract_fusion
  739.2 1.7 slice.237.refs_3_
  742.3 50.8 %ortho_last.1 = (f32[192,768]{1,0:T(8,128)}, f32[192,256]{1,0:T(8,128)}, f32[192,128]{1,0:T(8,128)}) custom-call(f32[256,768]{1,0:T(8,128)} %get-tuple-element.292.refs_0_, f32[256,512]{1,0:T(8,128)} %get-tuple-element.293.refs_1_, f32[256,256]{1,0:T(8,128)} %get-tuple-element.294.refs_2_, f32[256,256]{1,0:T(8,128)} %slice.237.refs_3_, ...), custom_call_target="tpu_custom_call" | custom-call | flops 40674263040 | tf_op jit(solution)/shard_map/ortho_last/pallas_call | solution.py:519
  793.9 5.4 all-gather
  804.1 1.6 multiply_subtract_fusion.4
  805.8 2.0 multiply_subtract_fusion.1
  808.5 1.4 multiply_subtract_fusion.3
  (389 shorter events, 58.4 us)
Async XLA Ops:
  7.2 407.5 %reduce-scatter.3.cloned.1.call-start = ((), (), s32[]{:S(2)}) async-start(), calls=%async_computation.2 | async-start | bytes 1966080 | tf_op jit(solution)/shard_map/reduce_scatter | solution.py:623
  12.8 66.7 %copy-start.103 = (f32[3,48]{1,0:T(4,128)S(1)}, f32[3,48]{1,0:T(4,128)}, u32[]{:S(2)}) copy-start(f32[3,48]{1,0:T(4,128)} %param.32) | copy-start | bytes 1732
  12.9 70.9 %copy-start.96 = (f32[192,12]{0,1:T(8,128)S(1)}, f32[192,12]{0,1:T(8,128)}, u32[]{:S(2)}) copy-start(f32[192,12]{0,1:T(8,128)} %param.37) | copy-start | bytes 27652
  12.9 74.0 %copy-start.82 = (f32[5,256]{1,0:T(8,128)S(1)}, f32[5,256]{1,0:T(8,128)}, u32[]{:S(2)}) copy-start(f32[5,256]{1,0:T(8,128)} %param.31) | copy-start | bytes 15364
  12.9 76.1 %copy-start.33 = (f32[1,256,1536]{2,1,0:T(8,128)S(1)}, f32[1,256,1536]{2,1,0:T(8,128)}, u32[]{:S(2)}) copy-start(f32[1,256,1536]{2,1,0:T(8,128)} %param.23) | copy-start | bytes 4718596
  75.5 23.3 %collective-permute-start = (f32[1,3,832]{2,1,0:T(4,128)}, f32[1,3,832]{2,1,0:T(4,128)}, u32[]{:S(2)}, u32[]{:S(2)}) collective-permute-start(f32[1,3,832]{2,1,0:T(4,128)} %slice.207), channel_id=1, source_target_pairs={{0,4},{4,8},{8,12},{12,16},{16,20},{20,24},{24,28},{1,5},{5,9},{9,... | collective-permute-start | bytes 29960 | tf_op jit(solution)/shard_map/ppermute | solution.py:37
  80.1 11.3 %copy-start.84 = (f32[12]{0:T(128)}, f32[12]{0:T(128)S(1)}, u32[]{:S(2)}) copy-start(f32[12]{0:T(128)S(1)} %get-tuple-element.352) | copy-start | bytes 148
  82.0 9.4 %copy-start.105 = (f32[12]{0:T(128)}, f32[12]{0:T(128)S(1)}, u32[]{:S(2)}) copy-start(f32[12]{0:T(128)S(1)} %get-tuple-element.347) | copy-start | bytes 148
  82.1 9.4 %copy-start.108 = (f32[12]{0:T(128)}, f32[12]{0:T(128)S(1)}, u32[]{:S(2)}) copy-start(f32[12]{0:T(128)S(1)} %get-tuple-element.346) | copy-start | bytes 148
  90.5 6.9 copy-start.119
  90.5 8.1 copy-start.55
  90.5 8.1 copy-start.95
  90.5 8.3 %copy-start.2 = (f32[256,896]{1,0:T(8,128)S(1)}, f32[256,896]{1,0:T(8,128)}, u32[]{:S(2)}) copy-start(f32[256,896]{1,0:T(8,128)} %get-tuple-element.53) | copy-start | bytes 2752516
  91.3 9.9 %copy-start.61 = (f32[256,12]{0,1:T(8,128)}, f32[256,12]{0,1:T(8,128)S(1)}, u32[]{:S(2)}) copy-start(f32[256,12]{0,1:T(8,128)S(1)} %copy.291) | copy-start | bytes 36868
  98.7 9.8 %copy-start.69 = (f32[832]{0:T(1024)}, f32[832]{0:T(1024)S(1)}, u32[]{:S(2)}) copy-start(f32[832]{0:T(1024)S(1)} %get-tuple-element.287) | copy-start | bytes 9988
  98.7 9.8 %copy-start.71 = (f32[832]{0:T(1024)}, f32[832]{0:T(1024)S(1)}, u32[]{:S(2)}) copy-start(f32[832]{0:T(1024)S(1)} %get-tuple-element.288) | copy-start | bytes 9988
  98.8 9.8 %copy-start.73 = (f32[832]{0:T(1024)}, f32[832]{0:T(1024)S(1)}, u32[]{:S(2)}) copy-start(f32[832]{0:T(1024)S(1)} %get-tuple-element.289) | copy-start | bytes 9988
  98.8 9.8 %copy-start.75 = (f32[832]{0:T(1024)}, f32[832]{0:T(1024)S(1)}, u32[]{:S(2)}) copy-start(f32[832]{0:T(1024)S(1)} %get-tuple-element.290) | copy-start | bytes 9988
  101.2 8.2 copy-start.52
  101.2 8.2 %copy-start.111 = (f32[12]{0:T(128)S(1)}, f32[12]{0:T(128)}, u32[]{:S(2)}) copy-start(f32[12]{0:T(128)} %get-tuple-element.349) | copy-start | bytes 148
  108.7 7.2 copy-start.20
  235.7 8.5 %copy-start.79 = (f32[1,256,1]{1,2,0:T(1,128)}, f32[1,256,1]{1,2,0:T(1,128)S(1)}, u32[]{:S(2)}) copy-start(f32[1,256,1]{1,2,0:T(1,128)S(1)} %get-tuple-element.320) | copy-start | bytes 3076
  259.3 7.3 copy-start.60
  264.9 182.7 %all-reduce.18.cloned.1.call-start = ((), (), s32[]{:S(2)}) async-start(), calls=%async_computation.4 | async-start | bytes 524288
  275.3 121.3 %copy-start.97 = (f32[768]{0:T(1024)S(1)}, f32[768]{0:T(1024)}, u32[]{:S(2)}) copy-start(f32[768]{0:T(1024)} %get-tuple-element.316) | copy-start | bytes 9220
  275.3 124.0 %copy-start.7 = (f32[256,768]{0,1:T(8,128)S(1)}, f32[256,768]{0,1:T(8,128)}, u32[]{:S(2)}) copy-start(f32[256,768]{0,1:T(8,128)} %copy.301) | copy-start | bytes 2359300
  399.3 12.1 %slice-start = ((s8[4718592]{0:T(1024)(128)(4,1)}), s8[4194304]{0:T(1024)(128)(4,1)S(1)}, s32[]{:S(2)}) async-start(s8[4718592]{0:T(1024)(128)(4,1)} %bitcast.323), calls=%async_computation.7 | async-start | bytes 8388608
  406.4 11.8 %copy-start.3 = (f32[192,768]{1,0:T(8,128)}, f32[192,768]{1,0:T(8,128)S(1)}, u32[]{:S(2)}) copy-start(f32[192,768]{1,0:T(8,128)S(1)} %multiply_add_fusion.1.refs_7_) | copy-start | bytes 1769476
  418.1 200.4 %all-reduce.22.cloned.1.call-start = ((), (), s32[]{:S(2)}) async-start(), calls=%async_computation.6 | async-start | bytes 6291456 | tf_op jit(solution)/shard_map/psum | solution.py:713
  419.4 319.8 %all-reduce.20.cloned.1.call-start = ((), (), s32[]{:S(2)}) async-start(), calls=%async_computation.5 | async-start | bytes 3768320 | tf_op jit(solution)/shard_map/psum | solution.py:718
  429.4 19.1 %copy-start.15 = (f32[1,256,832]{2,1,0:T(8,128)S(1)}, f32[1,256,832]{2,1,0:T(8,128)}, u32[]{:S(2)}) copy-start(f32[1,256,832]{2,1,0:T(8,128)} %get-tuple-element.325) | copy-start | bytes 2555908
  430.9 19.2 %copy-start.70 = (f32[832]{0:T(1024)S(1)}, f32[832]{0:T(1024)}, u32[]{:S(2)}) copy-start(f32[832]{0:T(1024)} %copy-done.69) | copy-start | bytes 9988
  430.9 19.2 %copy-start.72 = (f32[832]{0:T(1024)S(1)}, f32[832]{0:T(1024)}, u32[]{:S(2)}) copy-start(f32[832]{0:T(1024)} %copy-done.71) | copy-start | bytes 9988
  431.0 19.2 %copy-start.74 = (f32[832]{0:T(1024)S(1)}, f32[832]{0:T(1024)}, u32[]{:S(2)}) copy-start(f32[832]{0:T(1024)} %copy-done.73) | copy-start | bytes 9988
  431.0 19.2 %copy-start.76 = (f32[832]{0:T(1024)S(1)}, f32[832]{0:T(1024)}, u32[]{:S(2)}) copy-start(f32[832]{0:T(1024)} %copy-done.75) | copy-start | bytes 9988
  450.5 5.6 collective-permute-start.1
  555.7 66.6 %slice-start.2 = ((f32[192,896]{1,0:T(8,128)}), f32[192,64]{1,0:T(8,128)S(1)}, s32[]{:S(2)}) async-start(f32[192,896]{1,0:T(8,128)} %ring_scatter_3.1), calls=%async_computation.9 | async-start | bytes 196608 | tf_op jit(solution)/shard_map/slice | solution.py:690
  555.7 73.9 %copy-start.1 = (f32[1,256,1536]{1,2,0:T(8,128)S(1)}, f32[1,256,1536]{1,2,0:T(8,128)}, u32[]{:S(2)}) copy-start(f32[1,256,1536]{1,2,0:T(8,128)} %copy-done) | copy-start | bytes 4718596
  555.7 73.9 %copy-start.14 = (f32[256,896]{1,0:T(8,128)S(1)}, f32[256,896]{1,0:T(8,128)}, u32[]{:S(2)}) copy-start(f32[256,896]{1,0:T(8,128)} %maximum_bitcast_fusion.refs_1_) | copy-start | bytes 2752516
  555.7 73.9 %copy-start.58 = (f32[1536]{0:T(1024)S(1)}, f32[1536]{0:T(1024)}, u32[]{:S(2)}) copy-start(f32[1536]{0:T(1024)} %param.29) | copy-start | bytes 18436
  558.0 79.4 %copy-start.5 = (f32[192,768]{1,0:T(8,128)}, f32[192,768]{1,0:T(8,128)S(1)}, u32[]{:S(2)}) copy-start(f32[192,768]{1,0:T(8,128)S(1)} %get-tuple-element.417.refs_5_) | copy-start | bytes 1769476
  628.3 9.9 %copy-start.38 = (f32[192,256]{1,0:T(8,128)}, f32[192,256]{1,0:T(8,128)S(1)}, u32[]{:S(2)}) copy-start(f32[192,256]{1,0:T(8,128)S(1)} %copy.324) | copy-start | bytes 589828
  629.7 7.7 copy-start.59
  629.7 7.7 copy-start.89
  629.7 7.7 copy-start.113
  639.1 86.0 %copy-start.32 = (f32[192,256]{1,0:T(8,128)}, f32[192,256]{1,0:T(8,128)S(1)}, u32[]{:S(2)}) copy-start(f32[192,256]{1,0:T(8,128)S(1)} %multiply_add_fusion.4.refs_6_) | copy-start | bytes 589828
  640.4 84.8 %copy-start.40 = (f32[192,768]{1,0:T(8,128)S(1)}, f32[192,768]{1,0:T(8,128)}, u32[]{:S(2)}) copy-start(f32[192,768]{1,0:T(8,128)} %refs_2_.1) | copy-start | bytes 1769476
  640.4 88.8 %copy-start.110 = (f32[256]{0:T(256)S(1)}, f32[256]{0:T(256)}, u32[]{:S(2)}) copy-start(f32[256]{0:T(256)} %get-tuple-element.271) | copy-start | bytes 3076
  640.4 96.8 %copy-start.41 = (f32[768,192]{0,1:T(8,128)S(1)}, f32[768,192]{0,1:T(8,128)}, u32[]{:S(2)}) copy-start(f32[768,192]{0,1:T(8,128)} %param.28) | copy-start | bytes 1769476
  640.4 168.1 %reduce-scatter.5.cloned.1.call-start = ((), (), s32[]{:S(2)}) async-start(), calls=%async_computation.3 | async-start | bytes 1966080 | tf_op jit(solution)/shard_map/reduce_scatter | solution.py:753
  742.2 57.8 %copy-start.37 = (f32[192,12]{1,0:T(8,128)S(1)}, f32[192,12]{1,0:T(8,128)}, u32[]{:S(2)}) copy-start(f32[192,12]{1,0:T(8,128)} %copy-done.36) | copy-start | bytes 27652
  742.2 59.5 %copy-start.104 = (f32[3,48]{1,0:T(4,128)S(1)}, f32[3,48]{1,0:T(4,128)}, u32[]{:S(2)}) copy-start(f32[3,48]{1,0:T(4,128)} %param.32) | copy-start | bytes 1732
  742.2 59.5 %copy-start.115 = (f32[3,48]{1,0:T(4,128)S(1)}, f32[3,48]{1,0:T(4,128)}, u32[]{:S(2)}) copy-start(f32[3,48]{1,0:T(4,128)} %param.42) | copy-start | bytes 1732
  742.2 60.1 %copy-start.101 = (f32[1536]{0:T(1024)S(1)}, f32[1536]{0:T(1024)}, u32[]{:S(2)}) copy-start(f32[1536]{0:T(1024)} %param.39) | copy-start | bytes 18436
  742.2 60.7 %copy-start.83 = (f32[5,256]{1,0:T(8,128)S(1)}, f32[5,256]{1,0:T(8,128)}, u32[]{:S(2)}) copy-start(f32[5,256]{1,0:T(8,128)} %param.31) | copy-start | bytes 15364
  742.2 60.7 %copy-start.102 = (f32[5,256]{1,0:T(8,128)S(1)}, f32[5,256]{1,0:T(8,128)}, u32[]{:S(2)}) copy-start(f32[5,256]{1,0:T(8,128)} %param.41) | copy-start | bytes 15364
  742.2 61.3 %copy-start.81 = (f32[3072]{0:T(1024)S(1)}, f32[3072]{0:T(1024)}, u32[]{:S(2)}) copy-start(f32[3072]{0:T(1024)} %param.33) | copy-start | bytes 36868
  742.2 61.3 %copy-start.98 = (f32[3072]{0:T(1024)S(1)}, f32[3072]{0:T(1024)}, u32[]{:S(2)}) copy-start(f32[3072]{0:T(1024)} %param.43) | copy-start | bytes 36868
  742.2 61.9 %copy-start.47 = (f32[192,256]{1,0:T(8,128)S(1)}, f32[192,256]{1,0:T(8,128)}, u32[]{:S(2)}) copy-start(f32[192,256]{1,0:T(8,128)} %param.26) | copy-start | bytes 589828
  742.3 63.5 %copy-start.31 = (f32[192,768]{1,0:T(8,128)S(1)}, f32[192,768]{1,0:T(8,128)}, u32[]{:S(2)}) copy-start(f32[192,768]{1,0:T(8,128)} %param.25) | copy-start | bytes 1769476
  793.1 14.7 %copy-start.51 = (f32[5,3072]{1,0:T(8,128)S(1)}, f32[5,3072]{1,0:T(8,128)}, u32[]{:S(2)}) copy-start(f32[5,3072]{1,0:T(8,128)} %param.30) | copy-start | bytes 184324
  793.1 14.7 %copy-start.56 = (f32[5,3072]{1,0:T(8,128)S(1)}, f32[5,3072]{1,0:T(8,128)}, u32[]{:S(2)}) copy-start(f32[5,3072]{1,0:T(8,128)} %param.40) | copy-start | bytes 184324
  799.6 8.9 %copy-start.48 = (f32[4,5,768]{2,1,0:T(8,128)}, f32[4,5,768]{2,1,0:T(8,128)S(1)}, u32[]{:S(2)}) copy-start(f32[4,5,768]{2,1,0:T(8,128)S(1)} %slice.231) | copy-start | bytes 184324
  799.7 11.1 %copy-start.77 = (f32[5,256]{1,0:T(8,128)}, f32[5,256]{1,0:T(8,128)S(1)}, u32[]{:S(2)}) copy-start(f32[5,256]{1,0:T(8,128)S(1)} %reshape.824) | copy-start | bytes 15364
  (66 other events, 263.8 us)
Sparse Core Ops, SparseCore 0:
  265.0 36.0 reduce-scatter.2
  418.2 29.3 all-reduce.17
  453.0 165.4 all-reduce.21
  640.5 96.3 all-reduce.19
  739.3 27.3 reduce-scatter.4
